TPU v7x, 32 devices: a whole 2x2x4 slice. The times are simulated.
32 devices in a mesh: row: 16 (over z, y, core), col: 2 (over x).
Axes of the slice: x: 2, y: 2, z: 4, core: 2. Of those that a mesh axis runs over, the one named last changes fastest.
Arguments:
- vectors: float32 [1024, 32768], P(('row', 'col')), may hold values from -6 to 6
- reflectors: float32 [6, 128, 32768], P(None, 'col', 'row')
- factors: float32 [6, 128, 128], replicated, as said below
Outputs:
- transformed: float32 [1024, 32768], P('col', 'row')
Inputs may be any that keep to these rules, and one draw needn't show every extreme that they name: factors[k] is upper triangular, and its inverse equals the strict upper part of reflectors[k] reflectors[k]^T plus half of that product's diagonal, so each panel is orthogonal.
All inputs are finite; a program needn't handle non-finite values.
Results may differ from a plain program's by a relative error of at most 0.0001.
Values sent between devices are 32-bit elements; how exact they have to be, the bound alone decides.
No kernel may reach another device: no remote copies, remote signals or barrier semaphores. Data moves between devices by JAX's collectives and lax.ppermute only.
A program may use at most 128 MiB of HBM per device.

v0:
```python
import functools

import jax
import jax.numpy as jnp
from jax import lax
from jax.experimental import pallas as pl
from jax.experimental.pallas import tpu as pltpu
from jax.sharding import PartitionSpec as P


LOW_BITS = 2
TILE = 512
PROJECT_TILE = 1024


def outside(value):
    return pltpu.with_memory_space_constraint(value, pltpu.HBM)


def halves(value):
    high = value.astype(jnp.bfloat16)
    return high, (value - high.astype(jnp.float32)).astype(jnp.bfloat16)


def cut_kernel(length, flips, where_ref, source_ref, *refs):
    count = len(flips)
    outs, (held_ref, in_sem, out_sem) = refs[:count], refs[count:]
    loads = []
    for index in range(count):
        start = pl.multiple_of((where_ref[0] ^ flips[index]) * length, length)
        load = pltpu.make_async_copy(source_ref.at[:, pl.ds(start, length)], held_ref.at[index], in_sem.at[index])
        load.start()
        loads.append(load)
    stores = []
    for index in range(count):
        loads[index].wait()
        store = pltpu.make_async_copy(held_ref.at[index], outs[index], out_sem.at[index])
        store.start()
        stores.append(store)
    for store in stores:
        store.wait()


def cut(where, vectors, flips, length):
    rows, count = vectors.shape[0], len(flips)
    return pl.pallas_call(
        functools.partial(cut_kernel, length, flips),
        out_shape=[jax.ShapeDtypeStruct((rows, length), jnp.float32)] * count,
        grid_spec=pltpu.PrefetchScalarGridSpec(
            num_scalar_prefetch=1,
            grid=(),
            in_specs=[pl.BlockSpec(memory_space=pl.ANY)],
            out_specs=[pl.BlockSpec(memory_space=pl.ANY)] * count,
            scratch_shapes=[
                pltpu.VMEM((count, rows, length), jnp.float32),
                pltpu.SemaphoreType.DMA((count,)),
                pltpu.SemaphoreType.DMA((count,)),
            ],
        ),
        cost_estimate=pl.CostEstimate(
            flops=count * rows * length * 100, bytes_accessed=8 * count * rows * length, transcendentals=0
        ),
        compiler_params=pltpu.CompilerParams(vmem_limit_bytes=8 << 20),
        name="cut",
    )(where, vectors)


def across(left, right):
    return lax.dot_general(left, right, (((1,), (1,)), ((), ())), preferred_element_type=jnp.float32)


def prepare_kernel(plan, col_of, where_ref, *refs):
    col_count, width, steps = plan
    parts, (high_ref, low_ref, packed_ref, total_ref) = refs[:col_count], refs[col_count:]
    count, own_width = parts[0].shape[:2]
    col = col_of(where_ref[0])
    own_high, own_low = [], []
    for flip, part in enumerate(parts):
        for panel in range(count):
            high, low = halves(part[panel])
            start = pl.multiple_of(panel * width + (col ^ flip) * own_width, own_width)
            high_ref[pl.ds(start, own_width), :] = high
            low_ref[pl.ds(start, own_width), :] = low
            if flip == 0 and panel:
                own_high.append(high)
                own_low.append(low)
    own_high, own_low = jnp.concatenate(own_high, axis=0), jnp.concatenate(own_low, axis=0)
    before = (count - 1) * width
    value = across(own_high, high_ref[:before, :])
    value += across(own_high, low_ref[:before, :])
    value += across(own_low, high_ref[:before, :])

    @pl.when(pl.program_id(0) == 0)
    def _():
        total_ref[...] = value

    @pl.when(pl.program_id(0) > 0)
    def _():
        total_ref[...] += value

    @pl.when(pl.program_id(0) == steps - 1)
    def _():
        index = 0
        for second in range(1, count):
            for first in range(second):
                rows = slice((second - 1) * own_width, second * own_width)
                packed_ref[index * own_width : (index + 1) * own_width, :] = total_ref[
                    rows, first * width : (first + 1) * width
                ]
                index += 1
        packed_ref[index * own_width :, :] = jnp.zeros_like(packed_ref[index * own_width :, :])


def prepare(where, col_of, parts, packed_rows):
    count, own_width, length = parts[0].shape
    width = own_width * len(parts)
    tile = min(TILE, length)
    steps = length // tile
    return pl.pallas_call(
        functools.partial(prepare_kernel, (len(parts), width, steps), col_of),
        out_shape=[
            pltpu.HBM((count * width, length), jnp.bfloat16),
            pltpu.HBM((count * width, length), jnp.bfloat16),
            jax.ShapeDtypeStruct((packed_rows, width), jnp.float32),
        ],
        grid_spec=pltpu.PrefetchScalarGridSpec(
            num_scalar_prefetch=1,
            grid=(steps,),
            in_specs=[pl.BlockSpec((count, own_width, tile), lambda i, where: (0, 0, i)) for _ in parts],
            out_specs=[
                pl.BlockSpec((count * width, tile), lambda i, where: (0, i)),
                pl.BlockSpec((count * width, tile), lambda i, where: (0, i)),
                pl.BlockSpec((packed_rows, width), lambda i, where: (0, 0)),
            ],
            scratch_shapes=[pltpu.VMEM(((count - 1) * own_width, (count - 1) * width), jnp.float32)],
        ),
        cost_estimate=pl.CostEstimate(
            flops=6 * (count - 1) ** 2 * own_width * width * length,
            bytes_accessed=8 * count * width * length,
            transcendentals=0,
        ),
        compiler_params=pltpu.CompilerParams(vmem_limit_bytes=32 << 20),
        name="prepare",
    )(where, *[outside(part) for part in parts])


def project_kernel(plan, shift_of, where_ref, *refs):
    n_groups, n_rest, col_count, n_added, n_out, steps = plan
    pieces, refs = refs[: n_groups * n_rest], refs[n_groups * n_rest :]
    (high_ref, low_ref), added, refs = refs[:2], refs[2 : 2 + n_added], refs[2 + n_added :]
    outs, chosen, total_ref = refs[:n_out], refs[n_out:-1], refs[-1]
    shift = shift_of(where_ref[0])
    values = [piece[...] for piece in pieces]
    for group in range(n_groups):
        for flip in range(col_count):
            target = chosen[group * col_count + flip]
            for block in range(n_rest // col_count):
                value = values[group * n_rest + block]
                for high in range(1, col_count):
                    other = values[group * n_rest + high * (n_rest // col_count) + block]
                    value = jnp.where((shift ^ flip) == high, other, value)
                target[block] = value
    high, low = halves(jnp.concatenate(values, axis=0))
    size = high.shape[0]
    both = across(jnp.concatenate([high, low], axis=0), high_ref[...])
    value = both[:size] + both[size:] + across(high, low_ref[...])

    @pl.when(pl.program_id(0) == 0)
    def _():
        total_ref[...] = value

    @pl.when(pl.program_id(0) > 0)
    def _():
        total_ref[...] += value

    @pl.when(pl.program_id(0) == steps - 1)
    def _():
        share = size // n_out
        for index, out in enumerate(outs):
            result = total_ref[index * share : (index + 1) * share, :]
            for ref in added:
                result = result + ref[index * share : (index + 1) * share, :]
            out[...] = result


def project(where, shift_of, groups, high, low, added, col_count, n_out):
    pieces = [piece for group in groups for piece in group]
    n_rest = len(groups[0])
    rows, length = pieces[0].shape
    total = high.shape[0]
    tile = min(PROJECT_TILE, length)
    steps = length // tile
    size = len(pieces) * rows
    blocks = n_rest // col_count
    fixed = lambda i, where: (0, 0)
    moving = lambda i, where: (0, i)
    outs = pl.pallas_call(
        functools.partial(project_kernel, (len(groups), n_rest, col_count, len(added), n_out, steps), shift_of),
        out_shape=[jax.ShapeDtypeStruct((size // n_out, total), jnp.float32)] * n_out
        + [pltpu.HBM((blocks, rows, length), jnp.float32)] * (len(groups) * col_count),
        grid_spec=pltpu.PrefetchScalarGridSpec(
            num_scalar_prefetch=1,
            grid=(steps,),
            in_specs=[pl.BlockSpec((rows, tile), moving) for _ in pieces]
            + [pl.BlockSpec((total, tile), moving)] * 2
            + [pl.BlockSpec(value.shape, fixed) for value in added],
            out_specs=[pl.BlockSpec((size // n_out, total), fixed)] * n_out
            + [pl.BlockSpec((blocks, rows, tile), lambda i, where: (0, 0, i))] * (len(groups) * col_count),
            scratch_shapes=[pltpu.VMEM((size, total), jnp.float32)],
        ),
        cost_estimate=pl.CostEstimate(
            flops=6 * size * total * length, bytes_accessed=4 * (2 * size + total) * length, transcendentals=0
        ),
        compiler_params=pltpu.CompilerParams(vmem_limit_bytes=32 << 20),
        name="project",
    )(where, *[outside(piece) for piece in pieces], outside(high), outside(low), *added)
    chosen = outs[n_out:]
    return outs[:n_out], [chosen[g * col_count : (g + 1) * col_count] for g in range(len(groups))]


def factor_kernel(pair_rows, crossed_ref, factor_ref, high_ref, low_ref, whole_ref):
    count, width = factor_ref.shape[:2]
    col_count = crossed_ref.shape[0]

    def dot(left, right, axis):
        return lax.dot_general(
            left,
            right,
            (((1,), (axis,)), ((), ())),
            precision=lax.Precision.HIGHEST,
            preferred_element_type=jnp.float32,
        )

    whole_ref[...] = jnp.zeros_like(whole_ref)
    eye = (
        lax.broadcasted_iota(jnp.int32, (width, width), 0) == lax.broadcasted_iota(jnp.int32, (width, width), 1)
    ).astype(jnp.float32)
    for first in reversed(range(count)):
        at = slice(first * width, (first + 1) * width)
        factor = factor_ref[first]
        whole_ref[at, at] = dot(eye, factor, 1)
        if first < count - 1:
            inner = []
            for second in range(first + 1, count):
                pair = second * (second - 1) // 2 + first
                for col in range(col_count):
                    inner.append(crossed_ref[col, pair * pair_rows : (pair + 1) * pair_rows, :])
            inner = jnp.concatenate(inner, axis=0)
            after = (first + 1) * width
            whole_ref[after:, at] = -dot(dot(whole_ref[after:, after:], inner, 0), factor, 1)
    high, low = halves(whole_ref[...])
    high_ref[...] = high
    low_ref[...] = low


def factor(crossed, factors, pair_rows):
    count, width = factors.shape[:2]
    shape = jax.ShapeDtypeStruct((count * width, count * width), jnp.bfloat16)
    return pl.pallas_call(
        functools.partial(factor_kernel, pair_rows),
        out_shape=[shape, shape],
        scratch_shapes=[pltpu.VMEM((count * width, count * width), jnp.float32)],
        cost_estimate=pl.CostEstimate(flops=width**3 * count**3 * 4, bytes_accessed=1 << 22, transcendentals=0),
        compiler_params=pltpu.CompilerParams(vmem_limit_bytes=16 << 20),
        name="factor",
    )(crossed, factors)


def update_kernel(plan, place_of, where_ref, *refs):
    n_given, n_vector, rows = plan
    given, refs = refs[:n_given], refs[n_given:]
    vectors, refs = refs[:n_vector], refs[n_vector:]
    factor_high, factor_low, reflect_high, reflect_low, out_ref, high_ref, low_ref = refs
    places = place_of(where_ref[0])

    @pl.when(pl.program_id(0) == 0)
    def _():
        index = 0
        for ref in given:
            for block in range(ref.shape[0]):
                high, low = halves(ref[block])
                start = pl.multiple_of(places[index] * rows, rows)
                high_ref[pl.ds(start, rows), :] = high
                low_ref[pl.ds(start, rows), :] = low
                index += 1
        high = high_ref[...]
        update = jnp.dot(high, factor_high[...], preferred_element_type=jnp.float32)
        update += jnp.dot(high, factor_low[...], preferred_element_type=jnp.float32)
        update += jnp.dot(low_ref[...], factor_high[...], preferred_element_type=jnp.float32)
        high_ref[...], low_ref[...] = halves(update)

    high = high_ref[...]
    total = jnp.dot(high, reflect_high[...], preferred_element_type=jnp.float32)
    total += jnp.dot(high, reflect_low[...], preferred_element_type=jnp.float32)
    total += jnp.dot(low_ref[...], reflect_high[...], preferred_element_type=jnp.float32)
    out_ref[...] = total
    index = sum(ref.shape[0] for ref in given)
    for ref in vectors:
        for block in range(ref.shape[0]):
            start = pl.multiple_of(places[index] * rows, rows)
            out_ref[pl.ds(start, rows), :] = ref[block] - out_ref[pl.ds(start, rows), :]
            index += 1


def apply_update(where, place_of, given, vectors, factor_parts, reflect_parts, rows):
    total, length = reflect_parts[0].shape
    count = sum(value.shape[0] for value in given)
    tile = min(TILE, length)
    specs = [pl.BlockSpec(value.shape, lambda i, where: (0, 0, 0)) for value in given]
    specs += [pl.BlockSpec((value.shape[0], rows, tile), lambda i, where: (0, 0, i)) for value in vectors]
    specs += [pl.BlockSpec((total, total), lambda i, where: (0, 0))] * 2
    specs += [pl.BlockSpec((total, tile), lambda i, where: (0, i))] * 2
    return pl.pallas_call(
        functools.partial(update_kernel, (len(given), len(vectors), rows), place_of),
        out_shape=jax.ShapeDtypeStruct((count * rows, length), jnp.float32),
        grid_spec=pltpu.PrefetchScalarGridSpec(
            num_scalar_prefetch=1,
            grid=(length // tile,),
            in_specs=specs,
            out_specs=pl.BlockSpec((count * rows, tile), lambda i, where: (0, i)),
            scratch_shapes=[pltpu.VMEM((count * rows, total), jnp.bfloat16)] * 2,
        ),
        cost_estimate=pl.CostEstimate(
            flops=6 * count * rows * total * length,
            bytes_accessed=4 * (2 * count * rows * length + total * length + count * rows * total),
            transcendentals=0,
        ),
        compiler_params=pltpu.CompilerParams(vmem_limit_bytes=40 << 20),
        name="apply_update",
    )(where, *given, *map(outside, vectors), *factor_parts, *map(outside, reflect_parts))


def flipped(value, amount, axis, size):
    return jnp.stack([lax.dynamic_index_in_dim(value, i ^ amount, axis, keepdims=False) for i in range(size)], axis)


def transform(vectors, reflectors, factors):
    rows, whole_length = vectors.shape
    row_count = lax.axis_size("row")
    col_count = lax.axis_size("col")
    length = whole_length // row_count
    count, own_width = reflectors.shape[:2]
    width = own_width * col_count
    per_col = row_count // col_count
    low_bits = min(LOW_BITS, per_col.bit_length() - 1)
    groups = 1 << low_bits
    middle = per_col // groups
    rest_count = col_count * middle
    row = lax.axis_index("row")
    col = lax.axis_index("col")
    where = (row * col_count + col)[None]

    def flip_row(value, bits):
        return lax.ppermute(value, "row", [(i, i ^ bits) for i in range(row_count)])

    def flip_col(value, bits):
        return lax.ppermute(value, "col", [(i, i ^ bits) for i in range(col_count)])

    reflects = [reflectors]
    for flip in range(1, col_count):
        reflects.append(flip_col(reflectors, flip))

    group_order = list(reversed(range(groups)))
    pieces = {}
    for low in group_order:
        flips = [rest * groups + low for rest in reversed(range(rest_count))]
        cuts = cut(row[None], vectors, flips, length)
        arrived = []
        for flip, piece in zip(flips, cuts):
            arrived.append(flip_row(piece, flip) if flip else piece)
        pieces[low] = arrived[::-1]

    pairs = count * (count - 1) // 2
    share = -(-pairs * own_width // (row_count * 8)) * 8
    reflect_high, reflect_low, packed = prepare(where, lambda w: w % col_count, reflects, share * row_count)
    packed = packed.reshape(row_count, share, width)
    for bit in range(low_bits):
        mine = (row >> bit) & 1
        split = packed.reshape(packed.shape[0] // 2, 2, share, width)
        sent = lax.dynamic_index_in_dim(split, 1 - mine, 1, keepdims=False)
        kept = lax.dynamic_index_in_dim(split, mine, 1, keepdims=False)
        packed = kept + flip_row(sent, 1 << bit)
    rest_of = row // groups
    total = lax.dynamic_index_in_dim(packed, rest_of, 0, keepdims=False)
    for flip in range(1, rest_count):
        total = total + flip_row(lax.dynamic_index_in_dim(packed, rest_of ^ flip, 0, keepdims=False), flip * groups)
    both = [total]
    for flip in range(1, col_count):
        both.append(flip_col(total, flip))
    total = flipped(jnp.stack(both), col, 0, col_count)
    spread = [total]
    for flip in range(1, rest_count):
        spread.append(flip_row(total, flip * groups))
    spread = flipped(jnp.stack(spread), rest_of, 0, rest_count)
    for bit in reversed(range(low_bits)):
        mine = (row >> bit) & 1
        other = flip_row(spread, 1 << bit)
        spread = jnp.where(mine == 0, jnp.stack([spread, other], 1), jnp.stack([other, spread], 1))
        spread = spread.reshape(-1, col_count, share, width)
    crossed = jnp.swapaxes(spread, 0, 1).reshape(col_count, row_count * share, width)
    factor_parts = factor(crossed, factors, own_width)

    def shift_of(w):
        return (w // col_count // per_col) ^ (w % col_count)

    chosen = {}
    added = {low: [] for low in group_order}
    half = max(groups // 2, 1)
    for part in range(0, groups, half):
        lows = group_order[part : part + half]
        sums, kept = project(
            where, shift_of, [pieces[low] for low in lows], reflect_high, reflect_low, [], col_count, half
        )
        for low, value, kept_here in zip(lows, sums, kept):
            chosen[low] = kept_here
            for other in added[low]:
                value = value + other
            if low:
                bit = low.bit_length() - 1
                added[low ^ (1 << bit)].append(flip_row(value, 1 << bit))
    sums = value.reshape(rest_count, rows, count * width)

    moved = {}
    for low in group_order:
        for flip in range(1, col_count):
            moved[low, flip] = flip_col(chosen[low][flip], flip)

    projection = 0.0
    for high_flip in range(col_count):
        for middle_flip in range(middle):
            pairs_of = []
            for source_row in range(row_count):
                for source_col in range(col_count):
                    high = source_row // per_col
                    inside = (source_row % per_col) ^ (middle_flip * groups)
                    target = (source_col * per_col + inside) * col_count + (high ^ high_flip)
                    pairs_of.append((source_row * col_count + source_col, target))
            projection = projection + lax.ppermute(sums[high_flip * middle + middle_flip], ("row", "col"), pairs_of)

    gathered = {}
    first_group = []
    for high_flip in range(col_count):
        for middle_flip in range(middle):
            flip = high_flip * per_col + middle_flip * groups
            first_group.append(flip_row(projection, flip) if flip else projection)
    gathered[0] = jnp.stack(first_group)
    for bit in reversed(range(low_bits)):
        for low in list(gathered):
            gathered[low | (1 << bit)] = flip_row(gathered[low], 1 << bit)

    order = list(range(groups))
    keys = [(low, 0) for low in order] + [(low, flip) for low in order for flip in range(1, col_count)]

    def place_of(where):
        row, col = where // col_count, where % col_count
        low_of, middle_of, high_of = row % groups, (row // groups) % middle, row // per_col
        places = []
        for low in order:
            for high_flip in range(col_count):
                for middle_flip in range(middle):
                    inside = (middle_of ^ middle_flip) * groups + (low_of ^ low)
                    places.append(inside * col_count + (high_of ^ high_flip))
        for low, flip in keys:
            for middle_flip in range(middle):
                inside = (middle_of ^ middle_flip) * groups + (low_of ^ low)
                places.append(inside * col_count + (col ^ flip))
        return places

    return apply_update(
        where,
        place_of,
        [gathered[low] for low in order],
        [chosen[low][0] if flip == 0 else moved[low, flip] for low, flip in keys],
        factor_parts,
        (reflect_high, reflect_low),
        rows,
    )


def solution(mesh):
    return jax.shard_map(
        transform,
        mesh=mesh,
        in_specs=(P(("row", "col"), None), P(None, "col", "row"), P()),
        out_specs=P("col", "row"),
        check_vma=False,
    )
```

profile of v0, /device:TPU:0, one launch (start us, length us, event | category | flops | bytes accessed | tf_op | source)
XLA Modules:
  0.0 284.8 jit_solution(3152149588865593703)
XLA Ops:
  0.0 3.0 %collective-permute-start.7 = (f32[6,64,2048]{2,1,0:T(8,128)}, f32[6,64,2048]{2,1,0:T(8,128)}, u32[]{:S(2)}, u32[]{:S(2)}) collective-permute-start(f32[6,64,2048]{2,1,0:T(8,128)} %refs_0_.1), channel_id=1, source_target_pairs={{0,1},{1,0},{2,3},{3,2},{4,5},{5,4},{6,7},{7,6},{8,9},{9,8},{10,11... | collective-permute-start | bytes 9437192 | tf_op jit(solution)/shard_map/ppermute | solution.py:357
  7.7 63.7 %collective-permute-done.7.refs_1_ = f32[6,64,2048]{2,1,0:T(8,128)} collective-permute-done((f32[6,64,2048]{2,1,0:T(8,128)}, f32[6,64,2048]{2,1,0:T(8,128)}, u32[]{:S(2)}, u32[]{:S(2)}) %collective-permute-start.7) | collective-permute-done | bytes 3145760 | tf_op jit(solution)/shard_map/ppermute | solution.py:357
  71.4 8.6 %prepare.1 = (bf16[768,2048]{1,0:T(8,128)(2,1)}, bf16[768,2048]{1,0:T(8,128)(2,1)}, f32[1024,128]{1,0:T(8,128)S(1)}) custom-call(s32[1]{0:T(128)} %bitcast.where_ref, f32[6,64,2048]{2,1,0:T(8,128)} %refs_0_.1, f32[6,64,2048]{2,1,0:T(8,128)} %collective-permute-done.7.refs_1_), custom_call_target="tpu_custom_call" | custom-call | flops 2516582400 | bytes 12582912 | tf_op jit(solution)/shard_map/prepare/pallas_call | solution.py:119
  80.1 2.9 %collective-permute-start.5 = (f32[32,2048]{1,0:T(8,128)S(1)}, f32[32,2048]{1,0:T(8,128)S(1)}, u32[]{:S(2)}, u32[]{:S(2)}) collective-permute-start(f32[32,2048]{1,0:T(8,128)S(1)} %get-tuple-element.44), channel_id=1, source_target_pairs={{0,16},{2,18},{4,20},{6,22},{8,24},{10,26},{12,28},{14,30},{16,0},... | collective-permute-start | bytes 786440 | tf_op jit(solution)/shard_map/ppermute | solution.py:354
  86.3 3.8 %collective-permute-start.14 = (f32[32,2048]{1,0:T(8,128)S(1)}, f32[32,2048]{1,0:T(8,128)S(1)}, u32[]{:S(2)}, u32[]{:S(2)}) collective-permute-start(f32[32,2048]{1,0:T(8,128)S(1)} %get-tuple-element.55), channel_id=1, source_target_pairs={{0,20},{2,22},{4,16},{6,18},{8,28},{10,30},{12,24},{14,26},{16,4},... | collective-permute-start | bytes 786440 | tf_op jit(solution)/shard_map/ppermute | solution.py:354
  90.2 11.3 %collective-permute-done.5.refs_6_ = f32[32,2048]{1,0:T(8,128)S(1)} collective-permute-done((f32[32,2048]{1,0:T(8,128)S(1)}, f32[32,2048]{1,0:T(8,128)S(1)}, u32[]{:S(2)}, u32[]{:S(2)}) %collective-permute-start.5) | collective-permute-done | bytes 262176 | tf_op jit(solution)/shard_map/ppermute | solution.py:354
  105.7 3.5 %collective-permute-start.15 = (f32[32,2048]{1,0:T(8,128)S(1)}, f32[32,2048]{1,0:T(8,128)S(1)}, u32[]{:S(2)}, u32[]{:S(2)}) collective-permute-start(f32[32,2048]{1,0:T(8,128)S(1)} %get-tuple-element.56), channel_id=1, source_target_pairs={{0,28},{2,30},{4,24},{6,26},{8,20},{10,22},{12,16},{14,18},{16,12}... | collective-permute-start | bytes 786440 | tf_op jit(solution)/shard_map/ppermute | solution.py:354
  109.9 13.6 %collective-permute-start.9 = (f32[32,2048]{1,0:T(8,128)S(1)}, f32[32,2048]{1,0:T(8,128)}, u32[]{:S(2)}, u32[]{:S(2)}) collective-permute-start(f32[32,2048]{1,0:T(8,128)S(1)} %get-tuple-element.50), channel_id=1, source_target_pairs={{0,14},{2,12},{4,10},{6,8},{8,6},{10,4},{12,2},{14,0},{16,30},{18,... | collective-permute-start | bytes 786440 | tf_op jit(solution)/shard_map/ppermute | solution.py:354
  125.2 2.7 collective-permute-start.11
  128.0 20.2 %collective-permute-start.35 = (f32[64,128]{1,0:T(8,128)S(1)}, f32[64,128]{1,0:T(8,128)S(1)}, u32[]{:S(2)}, u32[]{:S(2)}) collective-permute-start(f32[64,128]{1,0:T(8,128)S(1)} %get-tuple-element.81), channel_id=1, source_target_pairs={{0,8},{2,10},{4,12},{6,14},{8,0},{10,2},{12,4},{14,6},{16,24},{18,... | collective-permute-start | bytes 98312 | tf_op jit(solution)/shard_map/ppermute | solution.py:354
  152.7 7.4 %collective-permute-start.2 = (f32[32,2048]{1,0:T(8,128)S(1)}, f32[32,2048]{1,0:T(8,128)S(1)}, u32[]{:S(2)}, u32[]{:S(2)}) collective-permute-start(f32[32,2048]{1,0:T(8,128)S(1)} %get-tuple-element.40), channel_id=1, source_target_pairs={{0,18},{2,16},{4,22},{6,20},{8,26},{10,24},{12,30},{14,28},{16,2},... | collective-permute-start | bytes 786440 | tf_op jit(solution)/shard_map/ppermute | solution.py:354
  161.3 6.5 %project.3 = (f32[128,768]{1,0:T(8,128)S(1)}, f32[128,768]{1,0:T(8,128)S(1)}, f32[2,32,2048]{2,1,0:T(8,128)}, f32[2,32,2048]{2,1,0:T(8,128)}, f32[2,32,2048]{2,1,0:T(8,128)}, /*index=5*/f32[2,32,2048]{2,1,0:T(8,128)}) custom-call(s32[1]{0:T(128)} %bitcast.where_ref, f32[32,2048]{1,0:T(8,128)} %copy-done.13, f32[32,2048]{1,0:T(8,128)} %collective-permute-done.9.refs_1_, ...), custom_call_target="tpu_custom_call" | custom-call | flops 2415919104 | bytes 10485760 | tf_op jit(solution)/shard_map/project/pallas_call | solution.py:197
  167.8 17.5 %collective-permute-done.36 = f32[64,128]{1,0:T(8,128)S(1)} collective-permute-done((f32[64,128]{1,0:T(8,128)S(1)}, f32[64,128]{1,0:T(8,128)S(1)}, u32[]{:S(2)}, u32[]{:S(2)}) %collective-permute-start.36) | collective-permute-done | bytes 32800 | tf_op jit(solution)/shard_map/ppermute | solution.py:354
  189.7 6.4 %project.2 = (f32[128,768]{1,0:T(8,128)S(1)}, f32[128,768]{1,0:T(8,128)S(1)}, f32[2,32,2048]{2,1,0:T(8,128)}, f32[2,32,2048]{2,1,0:T(8,128)}, f32[2,32,2048]{2,1,0:T(8,128)}, /*index=5*/f32[2,32,2048]{2,1,0:T(8,128)}) custom-call(s32[1]{0:T(128)} %bitcast.where_ref, f32[32,2048]{1,0:T(8,128)} %copy-done.14, f32[32,2048]{1,0:T(8,128)} %copy-done.15, ...), custom_call_target="tpu_custom_call" | custom-call | flops 2415919104 | bytes 10485760 | tf_op jit(solution)/shard_map/project/pallas_call | solution.py:197
  214.1 2.3 collective-permute-start.31
  216.4 8.8 %collective-permute-done.21 = f32[32,768]{1,0:T(8,128)S(1)} collective-permute-done((f32[32,768]{1,0:T(8,128)S(1)}, f32[32,768]{1,0:T(8,128)S(1)}, u32[]{:S(2)}, u32[]{:S(2)}) %collective-permute-start.21) | collective-permute-done | bytes 98336 | tf_op jit(solution)/shard_map/ppermute | solution.py:438
  225.2 4.0 %collective-permute-start.25 = (f32[32,768]{1,0:T(8,128)S(1)}, f32[32,768]{1,0:T(8,128)S(1)}, u32[]{:S(2)}, u32[]{:S(2)}) collective-permute-start(f32[32,768]{1,0:T(8,128)S(1)} %add_add_fusion.1), channel_id=1, source_target_pairs={{0,24},{2,26},{4,28},{6,30},{8,16},{10,18},{12,20},{14,22},{16,8},... | collective-permute-start | bytes 294920 | tf_op jit(solution)/shard_map/ppermute | solution.py:354
  230.0 2.9 %collective-permute-done.25 = f32[32,768]{1,0:T(8,128)S(1)} collective-permute-done((f32[32,768]{1,0:T(8,128)S(1)}, f32[32,768]{1,0:T(8,128)S(1)}, u32[]{:S(2)}, u32[]{:S(2)}) %collective-permute-start.25) | collective-permute-done | bytes 98336 | tf_op jit(solution)/shard_map/ppermute | solution.py:354
  232.9 3.1 %collective-permute-done.24 = f32[32,768]{1,0:T(8,128)S(1)} collective-permute-done((f32[32,768]{1,0:T(8,128)S(1)}, f32[32,768]{1,0:T(8,128)S(1)}, u32[]{:S(2)}, u32[]{:S(2)}) %collective-permute-start.24) | collective-permute-done | bytes 98336 | tf_op jit(solution)/shard_map/ppermute | solution.py:354
  240.8 6.3 %collective-permute-done.27.refs_2_ = f32[4,32,768]{2,1,0:T(8,128)S(1)} collective-permute-done((f32[4,32,768]{2,1,0:T(8,128)S(1)}, f32[4,32,768]{2,1,0:T(8,128)S(1)}, u32[]{:S(2)}, u32[]{:S(2)}) %collective-permute-start.27) | collective-permute-done | bytes 393248 | tf_op jit(solution)/shard_map/ppermute | solution.py:354
  248.4 7.6 %factor.1 = (bf16[768,768]{1,0:T(8,128)(2,1)S(1)}, bf16[768,768]{1,0:T(8,128)(2,1)S(1)}) custom-call(f32[2,1024,128]{2,1,0:T(8,128)S(1)} %bitcast.52, f32[6,128,128]{2,1,0:T(8,128)S(1)} %copy-done.4), custom_call_target="tpu_custom_call" | custom-call | flops 1811939328 | bytes 4194304 | tf_op jit(solution)/shard_map/factor/pallas_call | solution.py:259
  256.1 7.2 %collective-permute-done.29.refs_8_ = f32[2,32,2048]{2,1,0:T(8,128)} collective-permute-done((f32[2,32,2048]{2,1,0:T(8,128)}, f32[2,32,2048]{2,1,0:T(8,128)}, u32[]{:S(2)}, u32[]{:S(2)}) %collective-permute-start.29) | collective-permute-done | bytes 524320 | tf_op jit(solution)/shard_map/ppermute | solution.py:357
  263.3 9.7 %collective-permute-done.30.refs_9_ = f32[2,32,2048]{2,1,0:T(8,128)} collective-permute-done((f32[2,32,2048]{2,1,0:T(8,128)}, f32[2,32,2048]{2,1,0:T(8,128)}, u32[]{:S(2)}, u32[]{:S(2)}) %collective-permute-start.30) | collective-permute-done | bytes 524320 | tf_op jit(solution)/shard_map/ppermute | solution.py:357
  273.0 11.8 %apply_update.1 = f32[512,2048]{1,0:T(8,128)} custom-call(s32[1]{0:T(128)} %bitcast.where_ref, f32[4,32,768]{2,1,0:T(8,128)S(1)} %pad_maximum_fusion.refs_0_, f32[4,32,768]{2,1,0:T(8,128)S(1)} %collective-permute-done.26.refs_1_, f32[4,32,768]{2,1,0:T(8,128)S(1)} %collective-permute-done.27.refs_2_, f32[4,32,768]{2,1,0:T(8,128)S(1)} %collective-permute-done.28.refs_3_, ...), custom_call_target="tpu_custom_call" | custom-call | flops 4831838208 | bytes 16252928 | tf_op jit(solution)/shard_map/apply_update/pallas_call | solution.py:313
  (127 shorter events, 49.5 us)
Async XLA Ops:
  0.0 71.4 %collective-permute-start.7 = (f32[6,64,2048]{2,1,0:T(8,128)}, f32[6,64,2048]{2,1,0:T(8,128)}, u32[]{:S(2)}, u32[]{:S(2)}) collective-permute-start(f32[6,64,2048]{2,1,0:T(8,128)} %refs_0_.1), channel_id=1, source_target_pairs={{0,1},{1,0},{2,3},{3,2},{4,5},{5,4},{6,7},{7,6},{8,9},{9,8},{10,11... | collective-permute-start | bytes 9437192 | tf_op jit(solution)/shard_map/ppermute | solution.py:357
  6.1 80.1 %collective-permute-start.4 = (f32[32,2048]{1,0:T(8,128)S(1)}, f32[32,2048]{1,0:T(8,128)S(1)}, u32[]{:S(2)}, u32[]{:S(2)}) collective-permute-start(f32[32,2048]{1,0:T(8,128)S(1)} %get-tuple-element.43), channel_id=1, source_target_pairs={{0,8},{2,10},{4,12},{6,14},{8,0},{10,2},{12,4},{14,6},{16,24},{18,... | collective-permute-start | bytes 786440 | tf_op jit(solution)/shard_map/ppermute | solution.py:354
  80.1 21.4 %collective-permute-start.5 = (f32[32,2048]{1,0:T(8,128)S(1)}, f32[32,2048]{1,0:T(8,128)S(1)}, u32[]{:S(2)}, u32[]{:S(2)}) collective-permute-start(f32[32,2048]{1,0:T(8,128)S(1)} %get-tuple-element.44), channel_id=1, source_target_pairs={{0,16},{2,18},{4,20},{6,22},{8,24},{10,26},{12,28},{14,30},{16,0},... | collective-permute-start | bytes 786440 | tf_op jit(solution)/shard_map/ppermute | solution.py:354
  83.0 22.8 %collective-permute-start.6 = (f32[32,2048]{1,0:T(8,128)S(1)}, f32[32,2048]{1,0:T(8,128)}, u32[]{:S(2)}, u32[]{:S(2)}) collective-permute-start(f32[32,2048]{1,0:T(8,128)S(1)} %get-tuple-element.45), channel_id=1, source_target_pairs={{0,24},{2,26},{4,28},{6,30},{8,16},{10,18},{12,20},{14,22},{16,8},... | collective-permute-start | bytes 786440 | tf_op jit(solution)/shard_map/ppermute | solution.py:354
  84.6 24.7 %collective-permute-start.12 = (f32[32,2048]{1,0:T(8,128)S(1)}, f32[32,2048]{1,0:T(8,128)}, u32[]{:S(2)}, u32[]{:S(2)}) collective-permute-start(f32[32,2048]{1,0:T(8,128)S(1)} %get-tuple-element.53), channel_id=1, source_target_pairs={{0,4},{2,6},{4,0},{6,2},{8,12},{10,14},{12,8},{14,10},{16,20},{18,... | collective-permute-start | bytes 786440 | tf_op jit(solution)/shard_map/ppermute | solution.py:354
  86.2 23.7 %collective-permute-start.13 = (f32[32,2048]{1,0:T(8,128)S(1)}, f32[32,2048]{1,0:T(8,128)}, u32[]{:S(2)}, u32[]{:S(2)}) collective-permute-start(f32[32,2048]{1,0:T(8,128)S(1)} %get-tuple-element.54), channel_id=1, source_target_pairs={{0,12},{2,14},{4,8},{6,10},{8,4},{10,6},{12,0},{14,2},{16,28},{18,... | collective-permute-start | bytes 786440 | tf_op jit(solution)/shard_map/ppermute | solution.py:354
  86.3 38.8 %collective-permute-start.14 = (f32[32,2048]{1,0:T(8,128)S(1)}, f32[32,2048]{1,0:T(8,128)S(1)}, u32[]{:S(2)}, u32[]{:S(2)}) collective-permute-start(f32[32,2048]{1,0:T(8,128)S(1)} %get-tuple-element.55), channel_id=1, source_target_pairs={{0,20},{2,22},{4,16},{6,18},{8,28},{10,30},{12,24},{14,26},{16,4},... | collective-permute-start | bytes 786440 | tf_op jit(solution)/shard_map/ppermute | solution.py:354
  101.5 23.7 %collective-permute-start.34 = (f32[4,64,128]{2,1,0:T(8,128)S(1)}, f32[4,64,128]{2,1,0:T(8,128)S(1)}, u32[]{:S(2)}, u32[]{:S(2)}) collective-permute-start(f32[4,64,128]{2,1,0:T(8,128)S(1)} %dynamic-slice_bitcast_fusion.1), channel_id=1, source_target_pairs={{0,4},{2,6},{4,0},{6,2},{8,12},{10,14},{12,8},{14,10},{16,20},{18,... | collective-permute-start | bytes 393224 | tf_op jit(solution)/shard_map/ppermute | solution.py:354
  105.7 22.2 %collective-permute-start.15 = (f32[32,2048]{1,0:T(8,128)S(1)}, f32[32,2048]{1,0:T(8,128)S(1)}, u32[]{:S(2)}, u32[]{:S(2)}) collective-permute-start(f32[32,2048]{1,0:T(8,128)S(1)} %get-tuple-element.56), channel_id=1, source_target_pairs={{0,28},{2,30},{4,24},{6,26},{8,20},{10,22},{12,16},{14,18},{16,12}... | collective-permute-start | bytes 786440 | tf_op jit(solution)/shard_map/ppermute | solution.py:354
  109.3 38.9 %collective-permute-start.8 = (f32[32,2048]{1,0:T(8,128)S(1)}, f32[32,2048]{1,0:T(8,128)S(1)}, u32[]{:S(2)}, u32[]{:S(2)}) collective-permute-start(f32[32,2048]{1,0:T(8,128)S(1)} %get-tuple-element.49), channel_id=1, source_target_pairs={{0,6},{2,4},{4,2},{6,0},{8,14},{10,12},{12,10},{14,8},{16,22},{18,... | collective-permute-start | bytes 786440 | tf_op jit(solution)/shard_map/ppermute | solution.py:354
  109.9 42.5 %collective-permute-start.9 = (f32[32,2048]{1,0:T(8,128)S(1)}, f32[32,2048]{1,0:T(8,128)}, u32[]{:S(2)}, u32[]{:S(2)}) collective-permute-start(f32[32,2048]{1,0:T(8,128)S(1)} %get-tuple-element.50), channel_id=1, source_target_pairs={{0,14},{2,12},{4,10},{6,8},{8,6},{10,4},{12,2},{14,0},{16,30},{18,... | collective-permute-start | bytes 786440 | tf_op jit(solution)/shard_map/ppermute | solution.py:354
  125.2 27.5 %collective-permute-start.10 = (f32[32,2048]{1,0:T(8,128)S(1)}, f32[32,2048]{1,0:T(8,128)}, u32[]{:S(2)}, u32[]{:S(2)}) collective-permute-start(f32[32,2048]{1,0:T(8,128)S(1)} %get-tuple-element.51), channel_id=1, source_target_pairs={{0,22},{2,20},{4,18},{6,16},{8,30},{10,28},{12,26},{14,24},{16,6},... | collective-permute-start | bytes 786440 | tf_op jit(solution)/shard_map/ppermute | solution.py:354
  125.2 27.5 %collective-permute-start.11 = (f32[32,2048]{1,0:T(8,128)S(1)}, f32[32,2048]{1,0:T(8,128)}, u32[]{:S(2)}, u32[]{:S(2)}) collective-permute-start(f32[32,2048]{1,0:T(8,128)S(1)} %get-tuple-element.52), channel_id=1, source_target_pairs={{0,30},{2,28},{4,26},{6,24},{8,22},{10,20},{12,18},{14,16},{16,14}... | collective-permute-start | bytes 786440 | tf_op jit(solution)/shard_map/ppermute | solution.py:354
  128.0 32.2 %collective-permute-start.35 = (f32[64,128]{1,0:T(8,128)S(1)}, f32[64,128]{1,0:T(8,128)S(1)}, u32[]{:S(2)}, u32[]{:S(2)}) collective-permute-start(f32[64,128]{1,0:T(8,128)S(1)} %get-tuple-element.81), channel_id=1, source_target_pairs={{0,8},{2,10},{4,12},{6,14},{8,0},{10,2},{12,4},{14,6},{16,24},{18,... | collective-permute-start | bytes 98312 | tf_op jit(solution)/shard_map/ppermute | solution.py:354
  152.4 33.5 %collective-permute-start = (f32[32,2048]{1,0:T(8,128)S(1)}, f32[32,2048]{1,0:T(8,128)S(1)}, u32[]{:S(2)}, u32[]{:S(2)}) collective-permute-start(f32[32,2048]{1,0:T(8,128)S(1)} %get-tuple-element.38), channel_id=1, source_target_pairs={{0,2},{2,0},{4,6},{6,4},{8,10},{10,8},{12,14},{14,12},{16,18},{18,... | collective-permute-start | bytes 786440 | tf_op jit(solution)/shard_map/ppermute | solution.py:354
  152.7 34.7 %collective-permute-start.1 = (f32[32,2048]{1,0:T(8,128)S(1)}, f32[32,2048]{1,0:T(8,128)S(1)}, u32[]{:S(2)}, u32[]{:S(2)}) collective-permute-start(f32[32,2048]{1,0:T(8,128)S(1)} %get-tuple-element.39), channel_id=1, source_target_pairs={{0,10},{2,8},{4,14},{6,12},{8,2},{10,0},{12,6},{14,4},{16,26},{18,... | collective-permute-start | bytes 786440 | tf_op jit(solution)/shard_map/ppermute | solution.py:354
  152.7 36.2 %collective-permute-start.2 = (f32[32,2048]{1,0:T(8,128)S(1)}, f32[32,2048]{1,0:T(8,128)S(1)}, u32[]{:S(2)}, u32[]{:S(2)}) collective-permute-start(f32[32,2048]{1,0:T(8,128)S(1)} %get-tuple-element.40), channel_id=1, source_target_pairs={{0,18},{2,16},{4,22},{6,20},{8,26},{10,24},{12,30},{14,28},{16,2},... | collective-permute-start | bytes 786440 | tf_op jit(solution)/shard_map/ppermute | solution.py:354
  160.1 28.8 %collective-permute-start.3 = (f32[32,2048]{1,0:T(8,128)S(1)}, f32[32,2048]{1,0:T(8,128)S(1)}, u32[]{:S(2)}, u32[]{:S(2)}) collective-permute-start(f32[32,2048]{1,0:T(8,128)S(1)} %get-tuple-element.41), channel_id=1, source_target_pairs={{0,26},{2,24},{4,30},{6,28},{8,18},{10,16},{12,22},{14,20},{16,10}... | collective-permute-start | bytes 786440 | tf_op jit(solution)/shard_map/ppermute | solution.py:354
  161.3 24.0 %collective-permute-start.36 = (f32[64,128]{1,0:T(8,128)S(1)}, f32[64,128]{1,0:T(8,128)S(1)}, u32[]{:S(2)}, u32[]{:S(2)}) collective-permute-start(f32[64,128]{1,0:T(8,128)S(1)} %get-tuple-element.83), channel_id=1, source_target_pairs={{0,16},{2,18},{4,20},{6,22},{8,24},{10,26},{12,28},{14,30},{16,0},... | collective-permute-start | bytes 98312 | tf_op jit(solution)/shard_map/ppermute | solution.py:354
  214.1 24.9 %collective-permute-start.31 = (f32[2,32,2048]{2,1,0:T(8,128)S(1)}, f32[2,32,2048]{2,1,0:T(8,128)S(1)}, u32[]{:S(2)}, u32[]{:S(2)}) collective-permute-start(f32[2,32,2048]{2,1,0:T(8,128)S(1)} %copy-done.8), channel_id=1, source_target_pairs={{0,1},{1,0},{2,3},{3,2},{4,5},{5,4},{6,7},{7,6},{8,9},{9,8},{10,11... | collective-permute-start | bytes 1572872 | tf_op jit(solution)/shard_map/ppermute | solution.py:357
  238.8 24.5 %collective-permute-start.29 = (f32[2,32,2048]{2,1,0:T(8,128)}, f32[2,32,2048]{2,1,0:T(8,128)}, u32[]{:S(2)}, u32[]{:S(2)}) collective-permute-start(f32[2,32,2048]{2,1,0:T(8,128)} %get-tuple-element.64), channel_id=1, source_target_pairs={{0,1},{1,0},{2,3},{3,2},{4,5},{5,4},{6,7},{7,6},{8,9},{9,8},{10,11... | collective-permute-start | bytes 1572872 | tf_op jit(solution)/shard_map/ppermute | solution.py:357
  239.0 34.0 %collective-permute-start.30 = (f32[2,32,2048]{2,1,0:T(8,128)}, f32[2,32,2048]{2,1,0:T(8,128)}, u32[]{:S(2)}, u32[]{:S(2)}) collective-permute-start(f32[2,32,2048]{2,1,0:T(8,128)} %get-tuple-element.65), channel_id=1, source_target_pairs={{0,1},{1,0},{2,3},{3,2},{4,5},{5,4},{6,7},{7,6},{8,9},{9,8},{10,11... | collective-permute-start | bytes 1572872 | tf_op jit(solution)/shard_map/ppermute | solution.py:357
  240.8 32.2 %collective-permute-start.26 = (f32[4,32,768]{2,1,0:T(8,128)S(1)}, f32[4,32,768]{2,1,0:T(8,128)S(1)}, u32[]{:S(2)}, u32[]{:S(2)}) collective-permute-start(f32[4,32,768]{2,1,0:T(8,128)S(1)} %pad_maximum_fusion.refs_0_), channel_id=1, source_target_pairs={{0,2},{2,0},{4,6},{6,4},{8,10},{10,8},{12,14},{14,12},{16,18},{18,... | collective-permute-start | bytes 1179656 | tf_op jit(solution)/shard_map/ppermute | solution.py:354
  247.1 25.9 %collective-permute-start.28 = (f32[4,32,768]{2,1,0:T(8,128)S(1)}, f32[4,32,768]{2,1,0:T(8,128)S(1)}, u32[]{:S(2)}, u32[]{:S(2)}) collective-permute-start(f32[4,32,768]{2,1,0:T(8,128)S(1)} %collective-permute-done.27.refs_2_), channel_id=1, source_target_pairs={{0,2},{2,0},{4,6},{6,4},{8,10},{10,8},{12,14},{14,12},{16,18},{18,... | collective-permute-start | bytes 1179656 | tf_op jit(solution)/shard_map/ppermute | solution.py:354
  (38 other events, 512.8 us)
where the time goes:
time: 285 us
  waiting for transfers between devices  140 us (49%)
  starting transfers between devices  93 us (33%)
  Pallas kernels  41.8 us (15%)
  local copies, waits for them, and re-layouts  8.2 us (3%)
    ppermute x6, waiting for transfers between devices, flip_col(): return lax.ppermute(value, 'col', [(i, i ^ bits) for i in range(col_count)])  80.7 us
    ppermute x34, starting transfers between devices, flip_row(): return lax.ppermute(value, 'row', [(i, i ^ bits) for i in range(row_count)])  77 us
    ppermute x34, waiting for transfers between devices, flip_row(): return lax.ppermute(value, 'row', [(i, i ^ bits) for i in range(row_count)])  48.3 us
    pallas_call x2, Pallas kernels, project(): pl.pallas_call(functools.partial(project_kernel, (len(groups), n_rest, co...  12.9 us
    pallas_call x1, Pallas kernels, apply_update(): pl.pallas_call(functools.partial(update_kernel, (len(given), len(vectors)...  11.8 us
    ppermute x4, waiting for transfers between devices, transform(): lax.ppermute(sums[high_flip * middle + middle_flip], ('row', 'col'), pair...  10.7 us
    ppermute x6, starting transfers between devices, flip_col(): return lax.ppermute(value, 'col', [(i, i ^ bits) for i in range(col_count)])  10.6 us
    pallas_call x1, Pallas kernels, prepare(): pl.pallas_call(functools.partial(prepare_kernel, (len(parts), width, step...  8.58 us
  transfers between devices with their start and end apart: 44, of which 17 were waited for; matrix products, arithmetic and copies ran while one was open for 1% of the time, Pallas kernels for 11%

commit v1 on v0

--- a/solution.py
+++ b/solution.py
@@ -62,7 +62,7 @@
         ),
         compiler_params=pltpu.CompilerParams(vmem_limit_bytes=8 << 20),
         name="cut",
-    )(where, vectors)
+    )(where, outside(vectors))
 
 
 def across(left, right):
@@ -145,13 +145,13 @@
 
 
 def project_kernel(plan, shift_of, where_ref, *refs):
-    n_groups, n_rest, col_count, n_added, n_out, steps = plan
+    n_groups, n_rest, col_count, n_added, n_out, steps, choosing = plan
     pieces, refs = refs[: n_groups * n_rest], refs[n_groups * n_rest :]
     (high_ref, low_ref), added, refs = refs[:2], refs[2 : 2 + n_added], refs[2 + n_added :]
     outs, chosen, total_ref = refs[:n_out], refs[n_out:-1], refs[-1]
     shift = shift_of(where_ref[0])
     values = [piece[...] for piece in pieces]
-    for group in range(n_groups):
+    for group in range(n_groups if choosing else 0):
         for flip in range(col_count):
             target = chosen[group * col_count + flip]
             for block in range(n_rest // col_count):
@@ -183,7 +183,7 @@
             out[...] = result
 
 
-def project(where, shift_of, groups, high, low, added, col_count, n_out):
+def project(where, shift_of, groups, high, low, added, col_count, n_out, choosing):
     pieces = [piece for group in groups for piece in group]
     n_rest = len(groups[0])
     rows, length = pieces[0].shape
@@ -192,12 +192,13 @@
     steps = length // tile
     size = len(pieces) * rows
     blocks = n_rest // col_count
+    n_chosen = len(groups) * col_count if choosing else 0
     fixed = lambda i, where: (0, 0)
     moving = lambda i, where: (0, i)
     outs = pl.pallas_call(
-        functools.partial(project_kernel, (len(groups), n_rest, col_count, len(added), n_out, steps), shift_of),
+        functools.partial(project_kernel, (len(groups), n_rest, col_count, len(added), n_out, steps, choosing), shift_of),
         out_shape=[jax.ShapeDtypeStruct((size // n_out, total), jnp.float32)] * n_out
-        + [pltpu.HBM((blocks, rows, length), jnp.float32)] * (len(groups) * col_count),
+        + [pltpu.HBM((blocks, rows, length), jnp.float32)] * n_chosen,
         grid_spec=pltpu.PrefetchScalarGridSpec(
             num_scalar_prefetch=1,
             grid=(steps,),
@@ -205,7 +206,7 @@
             + [pl.BlockSpec((total, tile), moving)] * 2
             + [pl.BlockSpec(value.shape, fixed) for value in added],
             out_specs=[pl.BlockSpec((size // n_out, total), fixed)] * n_out
-            + [pl.BlockSpec((blocks, rows, tile), lambda i, where: (0, 0, i))] * (len(groups) * col_count),
+            + [pl.BlockSpec((blocks, rows, tile), lambda i, where: (0, 0, i))] * n_chosen,
             scratch_shapes=[pltpu.VMEM((size, total), jnp.float32)],
         ),
         cost_estimate=pl.CostEstimate(
@@ -215,7 +216,55 @@
         name="project",
     )(where, *[outside(piece) for piece in pieces], outside(high), outside(low), *added)
     chosen = outs[n_out:]
-    return outs[:n_out], [chosen[g * col_count : (g + 1) * col_count] for g in range(len(groups))]
+    return outs[:n_out], [chosen[g * col_count : (g + 1) * col_count] for g in range(len(groups) if choosing else 0)]
+
+
+def choose_kernel(col_count, shift_of, where_ref, *refs):
+    chosen, (held_ref, in_sem, out_sem) = refs[-3 - col_count : -3], refs[-3:]
+    pieces = refs[: -3 - col_count]
+    blocks = len(pieces) // col_count
+    shift = shift_of(where_ref[0])
+    loads = [pltpu.make_async_copy(piece, held_ref.at[i], in_sem.at[i]) for i, piece in enumerate(pieces)]
+    for load in loads:
+        load.start()
+    for load in loads:
+        load.wait()
+    stores = []
+    for flip in range(col_count):
+        for block in range(blocks):
+            source = (shift ^ flip) * blocks + block
+            stores.append(
+                pltpu.make_async_copy(held_ref.at[source], chosen[flip].at[block], out_sem.at[len(stores)])
+            )
+    for store in stores:
+        store.start()
+    for store in stores:
+        store.wait()
+
+
+def choose(where, shift_of, pieces, col_count):
+    rows, length = pieces[0].shape
+    anywhere = pl.BlockSpec(memory_space=pltpu.HBM)
+    return pl.pallas_call(
+        functools.partial(choose_kernel, col_count, shift_of),
+        out_shape=[pltpu.HBM((len(pieces) // col_count, rows, length), jnp.float32)] * col_count,
+        grid_spec=pltpu.PrefetchScalarGridSpec(
+            num_scalar_prefetch=1,
+            grid=(),
+            in_specs=[anywhere] * len(pieces),
+            out_specs=[anywhere] * col_count,
+            scratch_shapes=[
+                pltpu.VMEM((len(pieces), rows, length), jnp.float32),
+                pltpu.SemaphoreType.DMA((len(pieces),)),
+                pltpu.SemaphoreType.DMA((len(pieces),)),
+            ],
+        ),
+        cost_estimate=pl.CostEstimate(
+            flops=1 << 28, bytes_accessed=8 * len(pieces) * rows * length, transcendentals=0
+        ),
+        compiler_params=pltpu.CompilerParams(vmem_limit_bytes=8 << 20),
+        name="choose",
+    )(where, *[outside(piece) for piece in pieces])
 
 
 def factor_kernel(pair_rows, crossed_ref, factor_ref, high_ref, low_ref, whole_ref):
@@ -223,22 +272,19 @@
     col_count = crossed_ref.shape[0]
 
     def dot(left, right, axis):
-        return lax.dot_general(
-            left,
-            right,
-            (((1,), (axis,)), ((), ())),
-            precision=lax.Precision.HIGHEST,
-            preferred_element_type=jnp.float32,
-        )
+        def once(first, second):
+            return lax.dot_general(
+                first, second, (((1,), (axis,)), ((), ())), preferred_element_type=jnp.float32
+            )
+
+        (left_high, left_low), (right_high, right_low) = halves(left), halves(right)
+        return once(left_high, right_high) + once(left_high, right_low) + once(left_low, right_high)
 
     whole_ref[...] = jnp.zeros_like(whole_ref)
-    eye = (
-        lax.broadcasted_iota(jnp.int32, (width, width), 0) == lax.broadcasted_iota(jnp.int32, (width, width), 1)
-    ).astype(jnp.float32)
     for first in reversed(range(count)):
         at = slice(first * width, (first + 1) * width)
         factor = factor_ref[first]
-        whole_ref[at, at] = dot(eye, factor, 1)
+        whole_ref[at, at] = factor.T
         if first < count - 1:
             inner = []
             for second in range(first + 1, count):
@@ -267,11 +313,13 @@
 
 
 def update_kernel(plan, place_of, where_ref, *refs):
-    n_given, n_vector, rows = plan
+    n_given, n_vector, n_before, rows = plan
     given, refs = refs[:n_given], refs[n_given:]
     vectors, refs = refs[:n_vector], refs[n_vector:]
-    factor_high, factor_low, reflect_high, reflect_low, out_ref, high_ref, low_ref = refs
-    places = place_of(where_ref[0])
+    factor_high, factor_low, reflect_high, reflect_low = refs[:4]
+    out_ref, high_ref, low_ref = refs[4 + n_before :]
+    given_places, vector_places = place_of(where_ref[0])
+    middle, _, inner, tile = out_ref.shape
 
     @pl.when(pl.program_id(0) == 0)
     def _():
@@ -279,7 +327,7 @@
         for ref in given:
             for block in range(ref.shape[0]):
                 high, low = halves(ref[block])
-                start = pl.multiple_of(places[index] * rows, rows)
+                start = pl.multiple_of(given_places[index] * rows, rows)
                 high_ref[pl.ds(start, rows), :] = high
                 low_ref[pl.ds(start, rows), :] = low
                 index += 1
@@ -293,33 +341,38 @@
     total = jnp.dot(high, reflect_high[...], preferred_element_type=jnp.float32)
     total += jnp.dot(high, reflect_low[...], preferred_element_type=jnp.float32)
     total += jnp.dot(low_ref[...], reflect_high[...], preferred_element_type=jnp.float32)
-    out_ref[...] = total
-    index = sum(ref.shape[0] for ref in given)
+    out_ref[:, 0] = total.reshape(middle, inner, tile)
+    index = 0
     for ref in vectors:
         for block in range(ref.shape[0]):
-            start = pl.multiple_of(places[index] * rows, rows)
-            out_ref[pl.ds(start, rows), :] = ref[block] - out_ref[pl.ds(start, rows), :]
+            outer, place = vector_places[index]
+            at = (outer, 0, pl.ds(pl.multiple_of(place * rows, rows), rows))
+            out_ref[at] = ref[block] - out_ref[at]
             index += 1
 
 
-def apply_update(where, place_of, given, vectors, factor_parts, reflect_parts, rows):
+def apply_update(where, place_of, part_of, parts, middle, given, vectors, factor_parts, reflect_parts, before):
     total, length = reflect_parts[0].shape
+    rows = vectors[0].shape[1]
     count = sum(value.shape[0] for value in given)
+    inner = count * rows // middle
     tile = min(TILE, length)
     specs = [pl.BlockSpec(value.shape, lambda i, where: (0, 0, 0)) for value in given]
     specs += [pl.BlockSpec((value.shape[0], rows, tile), lambda i, where: (0, 0, i)) for value in vectors]
     specs += [pl.BlockSpec((total, total), lambda i, where: (0, 0))] * 2
     specs += [pl.BlockSpec((total, tile), lambda i, where: (0, i))] * 2
+    specs += [pl.BlockSpec(memory_space=pltpu.HBM)] * len(before)
     return pl.pallas_call(
-        functools.partial(update_kernel, (len(given), len(vectors), rows), place_of),
-        out_shape=jax.ShapeDtypeStruct((count * rows, length), jnp.float32),
+        functools.partial(update_kernel, (len(given), len(vectors), len(before), rows), place_of),
+        out_shape=jax.ShapeDtypeStruct((middle, parts, inner, length), jnp.float32),
         grid_spec=pltpu.PrefetchScalarGridSpec(
             num_scalar_prefetch=1,
             grid=(length // tile,),
             in_specs=specs,
-            out_specs=pl.BlockSpec((count * rows, tile), lambda i, where: (0, i)),
+            out_specs=pl.BlockSpec((middle, 1, inner, tile), lambda i, where: (0, part_of(where[0]), 0, i)),
             scratch_shapes=[pltpu.VMEM((count * rows, total), jnp.bfloat16)] * 2,
         ),
+        input_output_aliases={len(specs): 0} if before else {},
         cost_estimate=pl.CostEstimate(
             flops=6 * count * rows * total * length,
             bytes_accessed=4 * (2 * count * rows * length + total * length + count * rows * total),
@@ -327,7 +380,7 @@
         ),
         compiler_params=pltpu.CompilerParams(vmem_limit_bytes=40 << 20),
         name="apply_update",
-    )(where, *given, *map(outside, vectors), *factor_parts, *map(outside, reflect_parts))
+    )(where, *given, *map(outside, vectors), *factor_parts, *map(outside, reflect_parts), *before)
 
 
 def flipped(value, amount, axis, size):
@@ -369,6 +422,14 @@
         for flip, piece in zip(flips, cuts):
             arrived.append(flip_row(piece, flip) if flip else piece)
         pieces[low] = arrived[::-1]
+
+    def shift_of(w):
+        return (w // col_count // per_col) ^ (w % col_count)
+
+    half = max(groups // 2, 1)
+    chosen = {}
+    for low in group_order:
+        chosen[low] = choose(where, shift_of, pieces[low], col_count)
 
     pairs = count * (count - 1) // 2
     share = -(-pairs * own_width // (row_count * 8)) * 8
@@ -400,25 +461,31 @@
     crossed = jnp.swapaxes(spread, 0, 1).reshape(col_count, row_count * share, width)
     factor_parts = factor(crossed, factors, own_width)
 
-    def shift_of(w):
-        return (w // col_count // per_col) ^ (w % col_count)
-
-    chosen = {}
     added = {low: [] for low in group_order}
-    half = max(groups // 2, 1)
-    for part in range(0, groups, half):
-        lows = group_order[part : part + half]
-        sums, kept = project(
-            where, shift_of, [pieces[low] for low in lows], reflect_high, reflect_low, [], col_count, half
+    for lows in [group_order[:half]] + [[low] for low in group_order[half:]]:
+        sums, _ = project(
+            where,
+            shift_of,
+            [pieces[low] for low in lows],
+            reflect_high,
+            reflect_low,
+            [],
+            col_count,
+            len(lows),
+            False,
         )
-        for low, value, kept_here in zip(lows, sums, kept):
-            chosen[low] = kept_here
+        for low, value in zip(lows, sums):
             for other in added[low]:
                 value = value + other
             if low:
                 bit = low.bit_length() - 1
                 added[low ^ (1 << bit)].append(flip_row(value, 1 << bit))
-    sums = value.reshape(rest_count, rows, count * width)
+    value = value.reshape(col_count, middle, rows, count * width)
+    step = middle // 2
+    while step:
+        value = value[:, :step] + flip_row(value[:, step:], step * groups)
+        step //= 2
+    sums = value[:, 0]
 
     moved = {}
     for low in group_order:
@@ -427,15 +494,13 @@
 
     projection = 0.0
     for high_flip in range(col_count):
-        for middle_flip in range(middle):
-            pairs_of = []
-            for source_row in range(row_count):
-                for source_col in range(col_count):
-                    high = source_row // per_col
-                    inside = (source_row % per_col) ^ (middle_flip * groups)
-                    target = (source_col * per_col + inside) * col_count + (high ^ high_flip)
-                    pairs_of.append((source_row * col_count + source_col, target))
-            projection = projection + lax.ppermute(sums[high_flip * middle + middle_flip], ("row", "col"), pairs_of)
+        pairs_of = []
+        for source_row in range(row_count):
+            for source_col in range(col_count):
+                high, inside = source_row // per_col, source_row % per_col
+                target = (source_col * per_col + inside) * col_count + (high ^ high_flip)
+                pairs_of.append((source_row * col_count + source_col, target))
+        projection = projection + lax.ppermute(sums[high_flip], ("row", "col"), pairs_of)
 
     gathered = {}
     first_group = []
@@ -443,38 +508,61 @@
         for middle_flip in range(middle):
             flip = high_flip * per_col + middle_flip * groups
             first_group.append(flip_row(projection, flip) if flip else projection)
-    gathered[0] = jnp.stack(first_group)
+    gathered[0] = first_group
     for bit in reversed(range(low_bits)):
         for low in list(gathered):
-            gathered[low | (1 << bit)] = flip_row(gathered[low], 1 << bit)
-
-    order = list(range(groups))
-    keys = [(low, 0) for low in order] + [(low, flip) for low in order for flip in range(1, col_count)]
-
-    def place_of(where):
-        row, col = where // col_count, where % col_count
-        low_of, middle_of, high_of = row % groups, (row // groups) % middle, row // per_col
-        places = []
-        for low in order:
-            for high_flip in range(col_count):
-                for middle_flip in range(middle):
-                    inside = (middle_of ^ middle_flip) * groups + (low_of ^ low)
-                    places.append(inside * col_count + (high_of ^ high_flip))
-        for low, flip in keys:
-            for middle_flip in range(middle):
-                inside = (middle_of ^ middle_flip) * groups + (low_of ^ low)
-                places.append(inside * col_count + (col ^ flip))
+            blocks = gathered[low]
+            target = low | (1 << bit)
+            if bit:
+                sent = []
+                for block in blocks:
+                    sent.append(flip_row(block, 1 << bit))
+                gathered[target] = sent
+            else:
+                gathered[target] = [flip_row(jnp.stack(blocks), 1)]
+    gathered = {low: [b.reshape(-1, rows, count * width) for b in blocks] for low, blocks in gathered.items()}
+
+    parts = 1
+    per_part = groups // parts
+
+    def place_of(lows):
+        def places(where):
+            row, col = where // col_count, where % col_count
+            low_of, middle_of, high_of = row % groups, (row // groups) % middle, row // per_col
+            given_places, vector_places = [], []
+            for low in lows:
+                inside = (low_of ^ low) % per_part
+                for high_flip in range(col_count):
+                    for middle_flip in range(middle):
+                        given_places.append(
+                            ((middle_of ^ middle_flip) * per_part + inside) * col_count + (high_of ^ high_flip)
+                        )
+            for flip in range(col_count):
+                for low in lows:
+                    inside = (low_of ^ low) % per_part
+                    for middle_flip in range(middle):
+                        vector_places.append((middle_of ^ middle_flip, inside * col_count + (col ^ flip)))
+            return given_places, vector_places
+
         return places
 
-    return apply_update(
-        where,
-        place_of,
-        [gathered[low] for low in order],
-        [chosen[low][0] if flip == 0 else moved[low, flip] for low, flip in keys],
-        factor_parts,
-        (reflect_high, reflect_low),
-        rows,
-    )
+    before = ()
+    for part in range(parts):
+        lows = list(range(part * per_part, (part + 1) * per_part))
+        result = apply_update(
+            where,
+            place_of(lows),
+            lambda w, part=part: ((w // col_count) % groups) // per_part ^ part,
+            parts,
+            middle,
+            [block for low in lows for block in gathered[low]],
+            [chosen[low][0] if flip == 0 else moved[low, flip] for flip in range(col_count) for low in lows],
+            factor_parts,
+            (reflect_high, reflect_low),
+            before,
+        )
+        before = (result,)
+    return result.reshape(row_count * rows, length)
 
 
 def solution(mesh):

time: 285 us -> 290 us (1.018)
  Pallas kernels: 41.8 us -> 52.3 us
  starting transfers between devices: 93 us -> 86.3 us
  local copies, waits for them, and re-layouts: 8.2 us -> 3.95 us
  waiting for transfers between devices: 140 us -> 144 us
    ppermute x6, waiting for transfers between devices: 80.7 us -> 94.5 us  [flip_col(): return lax.ppermute(value, 'col', [(i, i ^ bits) for i in range(col_count)])]
    ppermute x4 -> x2, waiting for transfers between devices: 10.7 us -> 0.01 us  [transform(): lax.ppermute(sums[high_flip], ('row', 'col'), pairs_of)]
    pallas_call x0 -> x4, Pallas kernels: none -> 9.07 us  [choose(): pl.pallas_call(functools.partial(choose_kernel, col_count, shift_of), out...]
    ppermute x34 -> x38, starting transfers between devices: 77 us -> 70.4 us  [flip_row(): return lax.ppermute(value, 'row', [(i, i ^ bits) for i in range(row_count)])]
    unnamed x36 -> x50, local copies, waits for them, and re-layouts: 8.09 us -> 3.85 us
    pallas_call x4, Pallas kernels: 0.97 us -> 5.13 us  [cut(): pl.pallas_call(functools.partial(cut_kernel, length, flips), out_shape=[j...]
    pallas_call x1, Pallas kernels: 7.59 us -> 3.55 us  [factor(): pl.pallas_call(functools.partial(factor_kernel, pair_rows), out_shape=[sh...]
    ppermute x34 -> x38, waiting for transfers between devices: 48.3 us -> 49.9 us  [flip_row(): return lax.ppermute(value, 'row', [(i, i ^ bits) for i in range(row_count)])]
  transfers between devices with their start and end apart: 44 -> 46, of which waited for: 17 -> 11; matrix products, arithmetic and copies ran while one was open for 1% -> 1% of each run, Pallas kernels for 11% -> 11%
where the time goes in v1:
time: 290 us
  waiting for transfers between devices  144 us (50%)
  starting transfers between devices  86.3 us (30%)
  Pallas kernels  52.3 us (18%)
  local copies, waits for them, and re-layouts  3.95 us (1%)
    ppermute x6, waiting for transfers between devices, flip_col(): return lax.ppermute(value, 'col', [(i, i ^ bits) for i in range(col_count)])  94.5 us
    ppermute x38, starting transfers between devices, flip_row(): return lax.ppermute(value, 'row', [(i, i ^ bits) for i in range(row_count)])  70.4 us
    ppermute x38, waiting for transfers between devices, flip_row(): return lax.ppermute(value, 'row', [(i, i ^ bits) for i in range(row_count)])  49.9 us
    pallas_call x3, Pallas kernels, project(): pl.pallas_call(functools.partial(project_kernel, (len(groups), n_rest, co...  14.3 us
    ppermute x6, starting transfers between devices, flip_col(): return lax.ppermute(value, 'col', [(i, i ^ bits) for i in range(col_count)])  12.1 us
    pallas_call x1, Pallas kernels, apply_update(): pl.pallas_call(functools.partial(update_kernel, (len(given), len(vectors)...  11.8 us
    pallas_call x4, Pallas kernels, choose(): pl.pallas_call(functools.partial(choose_kernel, col_count, shift_of), out...  9.07 us
    pallas_call x1, Pallas kernels, prepare(): pl.pallas_call(functools.partial(prepare_kernel, (len(parts), width, step...  8.44 us
  transfers between devices with their start and end apart: 46, of which 11 were waited for; matrix products, arithmetic and copies ran while one was open for 1% of the time, Pallas kernels for 11%

profile of v1, /device:TPU:0, one launch (start us, length us, event | category | flops | bytes accessed | tf_op | source)
XLA Modules:
  0.0 289.6 jit_solution(14275580632561687903)
XLA Ops:
  0.0 3.0 %collective-permute-start.3 = (f32[6,64,2048]{2,1,0:T(8,128)}, f32[6,64,2048]{2,1,0:T(8,128)S(1)}, u32[]{:S(2)}, u32[]{:S(2)}) collective-permute-start(f32[6,64,2048]{2,1,0:T(8,128)} %refs_0_.1), channel_id=1, source_target_pairs={{0,1},{1,0},{2,3},{3,2},{4,5},{5,4},{6,7},{7,6},{8,9},{9,8},{10,11... | collective-permute-start | bytes 9437192 | tf_op jit(solution)/shard_map/ppermute | solution.py:410
  3.0 68.3 %collective-permute-done.3.refs_1_ = f32[6,64,2048]{2,1,0:T(8,128)S(1)} collective-permute-done((f32[6,64,2048]{2,1,0:T(8,128)}, f32[6,64,2048]{2,1,0:T(8,128)S(1)}, u32[]{:S(2)}, u32[]{:S(2)}) %collective-permute-start.3) | collective-permute-done | bytes 3145760 | tf_op jit(solution)/shard_map/ppermute | solution.py:410
  72.9 8.4 %prepare.1 = (bf16[768,2048]{1,0:T(8,128)(2,1)}, bf16[768,2048]{1,0:T(8,128)(2,1)}, f32[1024,128]{1,0:T(8,128)S(1)}) custom-call(s32[1]{0:T(128)} %bitcast.where_ref, f32[6,64,2048]{2,1,0:T(8,128)} %refs_0_.1, f32[6,64,2048]{2,1,0:T(8,128)} %copy-done.24), custom_call_target="tpu_custom_call" | custom-call | flops 2516582400 | bytes 12582912 | tf_op jit(solution)/shard_map/prepare/pallas_call | solution.py:119
  85.9 3.6 %collective-permute-start.6 = (f32[32,2048]{1,0:T(8,128)S(1)}, f32[32,2048]{1,0:T(8,128)S(1)}, u32[]{:S(2)}, u32[]{:S(2)}) collective-permute-start(f32[32,2048]{1,0:T(8,128)S(1)} %get-tuple-element.44), channel_id=1, source_target_pairs={{0,22},{2,20},{4,18},{6,16},{8,30},{10,28},{12,26},{14,24},{16,6},... | collective-permute-start | bytes 786440 | tf_op jit(solution)/shard_map/ppermute | solution.py:407
  91.9 16.3 %collective-permute-done.4.refs_0_ = f32[32,2048]{1,0:T(8,128)S(1)} collective-permute-done((f32[32,2048]{1,0:T(8,128)S(1)}, f32[32,2048]{1,0:T(8,128)S(1)}, u32[]{:S(2)}, u32[]{:S(2)}) %collective-permute-start.4) | collective-permute-done | bytes 262176 | tf_op jit(solution)/shard_map/ppermute | solution.py:407
  109.1 5.4 %collective-permute-start.10 = (f32[32,2048]{1,0:T(8,128)S(1)}, f32[32,2048]{1,0:T(8,128)S(1)}, u32[]{:S(2)}, u32[]{:S(2)}) collective-permute-start(f32[32,2048]{1,0:T(8,128)S(1)} %get-tuple-element.48), channel_id=1, source_target_pairs={{0,20},{2,22},{4,16},{6,18},{8,28},{10,30},{12,24},{14,26},{16,4},... | collective-permute-start | bytes 786440 | tf_op jit(solution)/shard_map/ppermute | solution.py:407
  116.1 17.8 %collective-permute-done.8.refs_4_.refs_0_ = f32[32,2048]{1,0:T(8,128)S(1)} collective-permute-done((f32[32,2048]{1,0:T(8,128)S(1)}, f32[32,2048]{1,0:T(8,128)S(1)}, u32[]{:S(2)}, u32[]{:S(2)}) %collective-permute-start.8) | collective-permute-done | bytes 262176 | tf_op jit(solution)/shard_map/ppermute | solution.py:407
  133.9 3.8 %collective-permute-start.39 = (f32[64,128]{1,0:T(8,128)S(1)}, f32[64,128]{1,0:T(8,128)S(1)}, u32[]{:S(2)}, u32[]{:S(2)}) collective-permute-start(f32[64,128]{1,0:T(8,128)S(1)} %get-tuple-element.76), channel_id=1, source_target_pairs={{0,24},{2,26},{4,28},{6,30},{8,16},{10,18},{12,20},{14,22},{16,8},... | collective-permute-start | bytes 98312 | tf_op jit(solution)/shard_map/ppermute | solution.py:407
  138.6 5.4 %project.4 = (f32[128,768]{1,0:T(8,128)S(1)}, f32[128,768]{1,0:T(8,128)S(1)}) custom-call(s32[1]{0:T(128)} %bitcast.where_ref, f32[32,2048]{1,0:T(8,128)} %copy-done.10, f32[32,2048]{1,0:T(8,128)} %copy-done.11, f32[32,2048]{1,0:T(8,128)} %copy-done.12, f32[32,2048]{1,0:T(8,128)} %copy-done.13, f32[32,2048]{1,0:T(8,128)} %copy-done.14, ...), custom_call_target="tpu_custom_call" | custom-call | flops 2415919104 | bytes 10485760 | tf_op jit(solution)/shard_map/project/pallas_call | solution.py:198
  154.1 6.3 %collective-permute-done.14.refs_1_ = f32[32,2048]{1,0:T(8,128)S(1)} collective-permute-done((f32[32,2048]{1,0:T(8,128)S(1)}, f32[32,2048]{1,0:T(8,128)S(1)}, u32[]{:S(2)}, u32[]{:S(2)}) %collective-permute-start.14) | collective-permute-done | bytes 262176 | tf_op jit(solution)/shard_map/ppermute | solution.py:407
  160.4 11.3 %collective-permute-start.2 = (f32[32,2048]{1,0:T(8,128)S(1)}, f32[32,2048]{1,0:T(8,128)S(1)}, u32[]{:S(2)}, u32[]{:S(2)}) collective-permute-start(f32[32,2048]{1,0:T(8,128)S(1)} %get-tuple-element.39), channel_id=1, source_target_pairs={{0,24},{2,26},{4,28},{6,30},{8,16},{10,18},{12,20},{14,22},{16,8},... | collective-permute-start | bytes 786440 | tf_op jit(solution)/shard_map/ppermute | solution.py:407
  173.2 4.4 %project.5 = f32[128,768]{1,0:T(8,128)S(1)} custom-call(s32[1]{0:T(128)} %bitcast.where_ref, f32[32,2048]{1,0:T(8,128)} %copy-done.2, f32[32,2048]{1,0:T(8,128)} %copy-done.3, f32[32,2048]{1,0:T(8,128)} %copy-done.4, f32[32,2048]{1,0:T(8,128)} %copy-done.5, bf16[768,2048]{1,0:T(8,128)(2,1)} %get-tuple-element.40.refs_4_.refs_8_.refs_20_, ...), custom_call_target="tpu_custom_call" | custom-call | flops 1207959552 | bytes 8388608 | tf_op jit(solution)/shard_map/project/pallas_call | solution.py:198
  178.8 16.0 %collective-permute-start.42 = (f32[2,64,128]{2,1,0:T(8,128)S(1)}, f32[2,64,128]{2,1,0:T(8,128)S(1)}, u32[]{:S(2)}, u32[]{:S(2)}) collective-permute-start(f32[2,64,128]{2,1,0:T(8,128)S(1)} %get-tuple-element.79), channel_id=1, source_target_pairs={{0,16},{2,18},{4,20},{6,22},{8,24},{10,26},{12,28},{14,30},{16,0},... | collective-permute-start | bytes 196616 | tf_op jit(solution)/shard_map/ppermute | solution.py:407
  196.3 4.4 %project.3 = f32[128,768]{1,0:T(8,128)S(1)} custom-call(s32[1]{0:T(128)} %bitcast.where_ref, f32[32,2048]{1,0:T(8,128)} %copy-done, f32[32,2048]{1,0:T(8,128)} %copy-done.6, f32[32,2048]{1,0:T(8,128)} %copy-done.7, f32[32,2048]{1,0:T(8,128)} %copy-done.8, bf16[768,2048]{1,0:T(8,128)(2,1)} %get-tuple-element.40.refs_4_.refs_8_.refs_20_, ...), custom_call_target="tpu_custom_call" | custom-call | flops 1207959552 | bytes 8388608 | tf_op jit(solution)/shard_map/project/pallas_call | solution.py:198
  201.5 4.5 %collective-permute-start.19 = (f32[2,1,32,768]{3,2,1,0:T(8,128)S(1)}, f32[2,1,32,768]{3,2,1,0:T(8,128)S(1)}, u32[]{:S(2)}, u32[]{:S(2)}) collective-permute-start(f32[2,1,32,768]{3,2,1,0:T(8,128)S(1)} %slice.19), channel_id=1, source_target_pairs={{0,8},{2,10},{4,12},{6,14},{8,0},{10,2},{12,4},{14,6},{16,24},{18,... | collective-permute-start | bytes 589832 | tf_op jit(solution)/shard_map/ppermute | solution.py:407
  215.8 3.5 %collective-permute-start.33 = (f32[2,32,2048]{2,1,0:T(8,128)}, f32[2,32,2048]{2,1,0:T(8,128)S(1)}, u32[]{:S(2)}, u32[]{:S(2)}) collective-permute-start(f32[2,32,2048]{2,1,0:T(8,128)} %get-tuple-element.62), channel_id=1, source_target_pairs={{0,1},{1,0},{2,3},{3,2},{4,5},{5,4},{6,7},{7,6},{8,9},{9,8},{10,11... | collective-permute-start | bytes 1572872 | tf_op jit(solution)/shard_map/ppermute | solution.py:410
  219.6 5.5 %collective-permute-start.24 = (f32[32,768]{1,0:T(8,128)S(1)}, f32[32,768]{1,0:T(8,128)S(1)}, u32[]{:S(2)}, u32[]{:S(2)}) collective-permute-start(f32[32,768]{1,0:T(8,128)S(1)} %add.80), channel_id=1, source_target_pairs={{0,24},{2,26},{4,28},{6,30},{8,16},{10,18},{12,20},{14,22},{16,8},... | collective-permute-start | bytes 294920 | tf_op jit(solution)/shard_map/ppermute | solution.py:407
  225.8 3.0 %collective-permute-done.24 = f32[32,768]{1,0:T(8,128)S(1)} collective-permute-done((f32[32,768]{1,0:T(8,128)S(1)}, f32[32,768]{1,0:T(8,128)S(1)}, u32[]{:S(2)}, u32[]{:S(2)}) %collective-permute-start.24) | collective-permute-done | bytes 98336 | tf_op jit(solution)/shard_map/ppermute | solution.py:407
  229.7 3.1 %collective-permute-done.23 = f32[32,768]{1,0:T(8,128)S(1)} collective-permute-done((f32[32,768]{1,0:T(8,128)S(1)}, f32[32,768]{1,0:T(8,128)S(1)}, u32[]{:S(2)}, u32[]{:S(2)}) %collective-permute-start.23) | collective-permute-done | bytes 98336 | tf_op jit(solution)/shard_map/ppermute | solution.py:407
  248.1 3.5 %factor.1 = (bf16[768,768]{1,0:T(8,128)(2,1)S(1)}, bf16[768,768]{1,0:T(8,128)(2,1)S(1)}) custom-call(f32[2,1024,128]{2,1,0:T(8,128)S(1)} %bitcast.62, f32[6,128,128]{2,1,0:T(8,128)S(1)} %copy-done.1), custom_call_target="tpu_custom_call" | custom-call | flops 1811939328 | bytes 4194304 | tf_op jit(solution)/shard_map/factor/pallas_call | solution.py:305
  251.6 5.3 %collective-permute-done.32.refs_15_ = f32[2,32,2048]{2,1,0:T(8,128)} collective-permute-done((f32[2,32,2048]{2,1,0:T(8,128)}, f32[2,32,2048]{2,1,0:T(8,128)}, u32[]{:S(2)}, u32[]{:S(2)}) %collective-permute-start.32) | collective-permute-done | bytes 524320 | tf_op jit(solution)/shard_map/ppermute | solution.py:410
  256.9 11.2 %collective-permute-done.31.refs_14_ = f32[2,32,2048]{2,1,0:T(8,128)} collective-permute-done((f32[2,32,2048]{2,1,0:T(8,128)}, f32[2,32,2048]{2,1,0:T(8,128)}, u32[]{:S(2)}, u32[]{:S(2)}) %collective-permute-start.31) | collective-permute-done | bytes 524320 | tf_op jit(solution)/shard_map/ppermute | solution.py:410
  268.1 9.6 %collective-permute-done.34.refs_17_ = f32[2,32,2048]{2,1,0:T(8,128)} collective-permute-done((f32[2,32,2048]{2,1,0:T(8,128)}, f32[2,32,2048]{2,1,0:T(8,128)}, u32[]{:S(2)}, u32[]{:S(2)}) %collective-permute-start.34) | collective-permute-done | bytes 524320 | tf_op jit(solution)/shard_map/ppermute | solution.py:410
  277.8 11.8 %apply_update.1 = f32[2,1,256,2048]{3,2,1,0:T(8,128)} custom-call(s32[1]{0:T(128)} %bitcast.where_ref, f32[1,32,768]{2,1,0:T(8,128)S(1)} %bitcast.64, f32[1,32,768]{2,1,0:T(8,128)S(1)} %bitcast.74, f32[1,32,768]{2,1,0:T(8,128)S(1)} %bitcast.72, f32[1,32,768]{2,1,0:T(8,128)S(1)} %bitcast.70, f32[4,32,768]{2,1,0:T(8,128)S(1)} %collective-permute-done.25.refs_4_, ...), custom_call_target="tpu_custom_call" | custom-call | flops 4831838208 | bytes 16252928 | tf_op jit(solution)/shard_map/apply_update/pallas_call | solution.py:365
  (153 shorter events, 53.5 us)
Async XLA Ops:
  0.0 71.3 %collective-permute-start.3 = (f32[6,64,2048]{2,1,0:T(8,128)}, f32[6,64,2048]{2,1,0:T(8,128)S(1)}, u32[]{:S(2)}, u32[]{:S(2)}) collective-permute-start(f32[6,64,2048]{2,1,0:T(8,128)} %refs_0_.1), channel_id=1, source_target_pairs={{0,1},{1,0},{2,3},{3,2},{4,5},{5,4},{6,7},{7,6},{8,9},{9,8},{10,11... | collective-permute-start | bytes 9437192 | tf_op jit(solution)/shard_map/ppermute | solution.py:410
  82.8 25.5 %collective-permute-start.4 = (f32[32,2048]{1,0:T(8,128)S(1)}, f32[32,2048]{1,0:T(8,128)S(1)}, u32[]{:S(2)}, u32[]{:S(2)}) collective-permute-start(f32[32,2048]{1,0:T(8,128)S(1)} %get-tuple-element.42), channel_id=1, source_target_pairs={{0,6},{2,4},{4,2},{6,0},{8,14},{10,12},{12,10},{14,8},{16,22},{18,... | collective-permute-start | bytes 786440 | tf_op jit(solution)/shard_map/ppermute | solution.py:407
  84.7 24.4 %collective-permute-start.5 = (f32[32,2048]{1,0:T(8,128)S(1)}, f32[32,2048]{1,0:T(8,128)S(1)}, u32[]{:S(2)}, u32[]{:S(2)}) collective-permute-start(f32[32,2048]{1,0:T(8,128)S(1)} %get-tuple-element.43), channel_id=1, source_target_pairs={{0,14},{2,12},{4,10},{6,8},{8,6},{10,4},{12,2},{14,0},{16,30},{18,... | collective-permute-start | bytes 786440 | tf_op jit(solution)/shard_map/ppermute | solution.py:407
  85.9 23.2 %collective-permute-start.6 = (f32[32,2048]{1,0:T(8,128)S(1)}, f32[32,2048]{1,0:T(8,128)S(1)}, u32[]{:S(2)}, u32[]{:S(2)}) collective-permute-start(f32[32,2048]{1,0:T(8,128)S(1)} %get-tuple-element.44), channel_id=1, source_target_pairs={{0,22},{2,20},{4,18},{6,16},{8,30},{10,28},{12,26},{14,24},{16,6},... | collective-permute-start | bytes 786440 | tf_op jit(solution)/shard_map/ppermute | solution.py:407
  89.6 24.9 %collective-permute-start.36 = (f32[4,64,128]{2,1,0:T(8,128)S(1)}, f32[4,64,128]{2,1,0:T(8,128)S(1)}, u32[]{:S(2)}, u32[]{:S(2)}) collective-permute-start(f32[4,64,128]{2,1,0:T(8,128)S(1)} %dynamic-slice_bitcast_fusion.1), channel_id=1, source_target_pairs={{0,4},{2,6},{4,0},{6,2},{8,12},{10,14},{12,8},{14,10},{16,20},{18,... | collective-permute-start | bytes 393224 | tf_op jit(solution)/shard_map/ppermute | solution.py:407
  90.1 25.8 %collective-permute-start.7 = (f32[32,2048]{1,0:T(8,128)S(1)}, f32[32,2048]{1,0:T(8,128)S(1)}, u32[]{:S(2)}, u32[]{:S(2)}) collective-permute-start(f32[32,2048]{1,0:T(8,128)S(1)} %get-tuple-element.45), channel_id=1, source_target_pairs={{0,30},{2,28},{4,26},{6,24},{8,22},{10,20},{12,18},{14,16},{16,14}... | collective-permute-start | bytes 786440 | tf_op jit(solution)/shard_map/ppermute | solution.py:407
  108.3 25.6 %collective-permute-start.8 = (f32[32,2048]{1,0:T(8,128)S(1)}, f32[32,2048]{1,0:T(8,128)S(1)}, u32[]{:S(2)}, u32[]{:S(2)}) collective-permute-start(f32[32,2048]{1,0:T(8,128)S(1)} %get-tuple-element.46), channel_id=1, source_target_pairs={{0,4},{2,6},{4,0},{6,2},{8,12},{10,14},{12,8},{14,10},{16,20},{18,... | collective-permute-start | bytes 786440 | tf_op jit(solution)/shard_map/ppermute | solution.py:407
  109.1 28.6 %collective-permute-start.9 = (f32[32,2048]{1,0:T(8,128)S(1)}, f32[32,2048]{1,0:T(8,128)S(1)}, u32[]{:S(2)}, u32[]{:S(2)}) collective-permute-start(f32[32,2048]{1,0:T(8,128)S(1)} %get-tuple-element.47), channel_id=1, source_target_pairs={{0,12},{2,14},{4,8},{6,10},{8,4},{10,6},{12,0},{14,2},{16,28},{18,... | collective-permute-start | bytes 786440 | tf_op jit(solution)/shard_map/ppermute | solution.py:407
  109.1 28.6 %collective-permute-start.10 = (f32[32,2048]{1,0:T(8,128)S(1)}, f32[32,2048]{1,0:T(8,128)S(1)}, u32[]{:S(2)}, u32[]{:S(2)}) collective-permute-start(f32[32,2048]{1,0:T(8,128)S(1)} %get-tuple-element.48), channel_id=1, source_target_pairs={{0,20},{2,22},{4,16},{6,18},{8,28},{10,30},{12,24},{14,26},{16,4},... | collective-permute-start | bytes 786440 | tf_op jit(solution)/shard_map/ppermute | solution.py:407
  114.5 23.3 %collective-permute-start.11 = (f32[32,2048]{1,0:T(8,128)S(1)}, f32[32,2048]{1,0:T(8,128)S(1)}, u32[]{:S(2)}, u32[]{:S(2)}) collective-permute-start(f32[32,2048]{1,0:T(8,128)S(1)} %get-tuple-element.49), channel_id=1, source_target_pairs={{0,28},{2,30},{4,24},{6,26},{8,20},{10,22},{12,16},{14,18},{16,12}... | collective-permute-start | bytes 786440 | tf_op jit(solution)/shard_map/ppermute | solution.py:407
  116.0 30.7 %collective-permute-start.37 = (f32[64,128]{1,0:T(8,128)S(1)}, f32[64,128]{1,0:T(8,128)S(1)}, u32[]{:S(2)}, u32[]{:S(2)}) collective-permute-start(f32[64,128]{1,0:T(8,128)S(1)} %get-tuple-element.75), channel_id=1, source_target_pairs={{0,8},{2,10},{4,12},{6,14},{8,0},{10,2},{12,4},{14,6},{16,24},{18,... | collective-permute-start | bytes 98312 | tf_op jit(solution)/shard_map/ppermute | solution.py:407
  144.1 33.5 %collective-permute-start.17 = (f32[128,768]{1,0:T(8,128)S(1)}, f32[128,768]{1,0:T(8,128)S(1)}, u32[]{:S(2)}, u32[]{:S(2)}) collective-permute-start(f32[128,768]{1,0:T(8,128)S(1)} %get-tuple-element.55), channel_id=1, source_target_pairs={{0,4},{2,6},{4,0},{6,2},{8,12},{10,14},{12,8},{14,10},{16,20},{18,... | collective-permute-start | bytes 1179656 | tf_op jit(solution)/shard_map/ppermute | solution.py:407
  153.5 25.2 %collective-permute-start = (f32[32,2048]{1,0:T(8,128)S(1)}, f32[32,2048]{1,0:T(8,128)S(1)}, u32[]{:S(2)}, u32[]{:S(2)}) collective-permute-start(f32[32,2048]{1,0:T(8,128)S(1)} %get-tuple-element.37), channel_id=1, source_target_pairs={{0,8},{2,10},{4,12},{6,14},{8,0},{10,2},{12,4},{14,6},{16,24},{18,... | collective-permute-start | bytes 786440 | tf_op jit(solution)/shard_map/ppermute | solution.py:407
  160.4 34.4 %collective-permute-start.1 = (f32[32,2048]{1,0:T(8,128)S(1)}, f32[32,2048]{1,0:T(8,128)S(1)}, u32[]{:S(2)}, u32[]{:S(2)}) collective-permute-start(f32[32,2048]{1,0:T(8,128)S(1)} %get-tuple-element.38), channel_id=1, source_target_pairs={{0,16},{2,18},{4,20},{6,22},{8,24},{10,26},{12,28},{14,30},{16,0},... | collective-permute-start | bytes 786440 | tf_op jit(solution)/shard_map/ppermute | solution.py:407
  160.4 34.4 %collective-permute-start.2 = (f32[32,2048]{1,0:T(8,128)S(1)}, f32[32,2048]{1,0:T(8,128)S(1)}, u32[]{:S(2)}, u32[]{:S(2)}) collective-permute-start(f32[32,2048]{1,0:T(8,128)S(1)} %get-tuple-element.39), channel_id=1, source_target_pairs={{0,24},{2,26},{4,28},{6,30},{8,16},{10,18},{12,20},{14,22},{16,8},... | collective-permute-start | bytes 786440 | tf_op jit(solution)/shard_map/ppermute | solution.py:407
  177.6 23.8 %collective-permute-start.12 = (f32[128,768]{1,0:T(8,128)S(1)}, f32[128,768]{1,0:T(8,128)S(1)}, u32[]{:S(2)}, u32[]{:S(2)}) collective-permute-start(f32[128,768]{1,0:T(8,128)S(1)} %get-tuple-element.50), channel_id=1, source_target_pairs={{0,4},{2,6},{4,0},{6,2},{8,12},{10,14},{12,8},{14,10},{16,20},{18,... | collective-permute-start | bytes 1179656 | tf_op jit(solution)/shard_map/ppermute | solution.py:407
  178.7 22.8 %collective-permute-start.18 = (f32[128,768]{1,0:T(8,128)S(1)}, f32[128,768]{1,0:T(8,128)S(1)}, u32[]{:S(2)}, u32[]{:S(2)}) collective-permute-start(f32[128,768]{1,0:T(8,128)S(1)} %add.77), channel_id=1, source_target_pairs={{0,2},{2,0},{4,6},{6,4},{8,10},{10,8},{12,14},{14,12},{16,18},{18,... | collective-permute-start | bytes 1179656 | tf_op jit(solution)/shard_map/ppermute | solution.py:407
  178.8 21.9 %collective-permute-start.42 = (f32[2,64,128]{2,1,0:T(8,128)S(1)}, f32[2,64,128]{2,1,0:T(8,128)S(1)}, u32[]{:S(2)}, u32[]{:S(2)}) collective-permute-start(f32[2,64,128]{2,1,0:T(8,128)S(1)} %get-tuple-element.79), channel_id=1, source_target_pairs={{0,16},{2,18},{4,20},{6,22},{8,24},{10,26},{12,28},{14,30},{16,0},... | collective-permute-start | bytes 196616 | tf_op jit(solution)/shard_map/ppermute | solution.py:407
  215.8 31.7 %collective-permute-start.33 = (f32[2,32,2048]{2,1,0:T(8,128)}, f32[2,32,2048]{2,1,0:T(8,128)S(1)}, u32[]{:S(2)}, u32[]{:S(2)}) collective-permute-start(f32[2,32,2048]{2,1,0:T(8,128)} %get-tuple-element.62), channel_id=1, source_target_pairs={{0,1},{1,0},{2,3},{3,2},{4,5},{5,4},{6,7},{7,6},{8,9},{9,8},{10,11... | collective-permute-start | bytes 1572872 | tf_op jit(solution)/shard_map/ppermute | solution.py:410
  219.6 27.9 %collective-permute-start.45 = (f32[8,2,64,128]{3,2,0,1:T(8,128)S(1)}, f32[8,2,64,128]{3,2,0,1:T(8,128)S(1)}, u32[]{:S(2)}, u32[]{:S(2)}) collective-permute-start(f32[8,2,64,128]{3,2,0,1:T(8,128)S(1)} %bitcast.81), channel_id=1, source_target_pairs={{0,2},{2,0},{4,6},{6,4},{8,10},{10,8},{12,14},{14,12},{16,18},{18,... | collective-permute-start | bytes 1572872 | tf_op jit(solution)/shard_map/ppermute | solution.py:407
  243.8 24.3 %collective-permute-start.31 = (f32[2,32,2048]{2,1,0:T(8,128)}, f32[2,32,2048]{2,1,0:T(8,128)}, u32[]{:S(2)}, u32[]{:S(2)}) collective-permute-start(f32[2,32,2048]{2,1,0:T(8,128)} %get-tuple-element.60), channel_id=1, source_target_pairs={{0,1},{1,0},{2,3},{3,2},{4,5},{5,4},{6,7},{7,6},{8,9},{9,8},{10,11... | collective-permute-start | bytes 1572872 | tf_op jit(solution)/shard_map/ppermute | solution.py:410
  243.9 33.9 %collective-permute-start.34 = (f32[2,32,2048]{2,1,0:T(8,128)}, f32[2,32,2048]{2,1,0:T(8,128)}, u32[]{:S(2)}, u32[]{:S(2)}) collective-permute-start(f32[2,32,2048]{2,1,0:T(8,128)} %get-tuple-element.63), channel_id=1, source_target_pairs={{0,1},{1,0},{2,3},{3,2},{4,5},{5,4},{6,7},{7,6},{8,9},{9,8},{10,11... | collective-permute-start | bytes 1572872 | tf_op jit(solution)/shard_map/ppermute | solution.py:410
  247.4 30.3 %collective-permute-start.25 = (f32[4,32,768]{2,1,0:T(8,128)}, f32[4,32,768]{2,1,0:T(8,128)S(1)}, u32[]{:S(2)}, u32[]{:S(2)}) collective-permute-start(f32[4,32,768]{2,1,0:T(8,128)} %pad_maximum_fusion), channel_id=1, source_target_pairs={{0,2},{2,0},{4,6},{6,4},{8,10},{10,8},{12,14},{14,12},{16,18},{18,... | collective-permute-start | bytes 1179656 | tf_op jit(solution)/shard_map/ppermute | solution.py:407
  247.5 30.3 %collective-permute-start.30 = (f32[4,32,768]{2,1,0:T(8,128)}, f32[4,32,768]{2,1,0:T(8,128)S(1)}, u32[]{:S(2)}, u32[]{:S(2)}) collective-permute-start(f32[4,32,768]{2,1,0:T(8,128)} %pad_maximum_fusion.1), channel_id=1, source_target_pairs={{0,2},{2,0},{4,6},{6,4},{8,10},{10,8},{12,14},{14,12},{16,18},{18,... | collective-permute-start | bytes 1179656 | tf_op jit(solution)/shard_map/ppermute | solution.py:407
  (47 other events, 439.8 us)

commit v2 on v1

--- a/solution.py
+++ b/solution.py
@@ -15,6 +15,10 @@
 
 def outside(value):
     return pltpu.with_memory_space_constraint(value, pltpu.HBM)
+
+
+def chunked(total, step):
+    return [slice(start, min(start + step, total)) for start in range(0, total, step)]
 
 
 def halves(value):
@@ -331,11 +335,12 @@
                 high_ref[pl.ds(start, rows), :] = high
                 low_ref[pl.ds(start, rows), :] = low
                 index += 1
-        high = high_ref[...]
-        update = jnp.dot(high, factor_high[...], preferred_element_type=jnp.float32)
-        update += jnp.dot(high, factor_low[...], preferred_element_type=jnp.float32)
-        update += jnp.dot(low_ref[...], factor_high[...], preferred_element_type=jnp.float32)
-        high_ref[...], low_ref[...] = halves(update)
+        for at in chunked(high_ref.shape[1], 256):
+            after = slice(at.start, None)
+            update = jnp.dot(high_ref[:, after], factor_high[after, at], preferred_element_type=jnp.float32)
+            update += jnp.dot(high_ref[:, after], factor_low[after, at], preferred_element_type=jnp.float32)
+            update += jnp.dot(low_ref[:, after], factor_high[after, at], preferred_element_type=jnp.float32)
+            high_ref[:, at], low_ref[:, at] = halves(update)
 
     high = high_ref[...]
     total = jnp.dot(high, reflect_high[...], preferred_element_type=jnp.float32)
@@ -380,7 +385,7 @@
         ),
         compiler_params=pltpu.CompilerParams(vmem_limit_bytes=40 << 20),
         name="apply_update",
-    )(where, *given, *map(outside, vectors), *factor_parts, *map(outside, reflect_parts), *before)
+    )(where, *given, *map(outside, vectors), *factor_parts, reflect_parts[0], outside(reflect_parts[1]), *before)
 
 
 def flipped(value, amount, axis, size):
@@ -478,7 +483,7 @@
             for other in added[low]:
                 value = value + other
             if low:
-                bit = low.bit_length() - 1
+                bit = (low & -low).bit_length() - 1
                 added[low ^ (1 << bit)].append(flip_row(value, 1 << bit))
     value = value.reshape(col_count, middle, rows, count * width)
     step = middle // 2

time: 290 us -> 290 us (level)
  no operation moved by 1% of the time
where the time goes in v2:
time: 290 us
  waiting for transfers between devices  145 us (50%)
  starting transfers between devices  86.7 us (30%)
  Pallas kernels  51.3 us (18%)
  local copies, waits for them, and re-layouts  4 us (1%)
    ppermute x6, waiting for transfers between devices, flip_col(): return lax.ppermute(value, 'col', [(i, i ^ bits) for i in range(col_count)])  94.4 us
    ppermute x38, starting transfers between devices, flip_row(): return lax.ppermute(value, 'row', [(i, i ^ bits) for i in range(row_count)])  70.6 us
    ppermute x38, waiting for transfers between devices, flip_row(): return lax.ppermute(value, 'row', [(i, i ^ bits) for i in range(row_count)])  50.6 us
    pallas_call x3, Pallas kernels, project(): pl.pallas_call(functools.partial(project_kernel, (len(groups), n_rest, co...  14.3 us
    ppermute x6, starting transfers between devices, flip_col(): return lax.ppermute(value, 'col', [(i, i ^ bits) for i in range(col_count)])  13.1 us
    pallas_call x1, Pallas kernels, apply_update(): pl.pallas_call(functools.partial(update_kernel, (len(given), len(vectors)...  10.8 us
    pallas_call x4, Pallas kernels, choose(): pl.pallas_call(functools.partial(choose_kernel, col_count, shift_of), out...  9.07 us
    pallas_call x1, Pallas kernels, prepare(): pl.pallas_call(functools.partial(prepare_kernel, (len(parts), width, step...  8.5 us
  transfers between devices with their start and end apart: 46, of which 11 were waited for; matrix products, arithmetic and copies ran while one was open for 1% of the time, Pallas kernels for 11%

profile of v2, /device:TPU:0, one launch (start us, length us, event | category | flops | bytes accessed | tf_op | source)
XLA Modules:
  0.0 289.7 jit_solution(8988155448535188202)
XLA Ops:
  3.0 68.3 %collective-permute-done.3.refs_1_ = f32[6,64,2048]{2,1,0:T(8,128)S(1)} collective-permute-done((f32[6,64,2048]{2,1,0:T(8,128)}, f32[6,64,2048]{2,1,0:T(8,128)S(1)}, u32[]{:S(2)}, u32[]{:S(2)}) %collective-permute-start.3) | collective-permute-done | bytes 3145760 | tf_op jit(solution)/shard_map/ppermute | solution.py:415
  72.9 8.5 %prepare.1 = (bf16[768,2048]{1,0:T(8,128)(2,1)}, bf16[768,2048]{1,0:T(8,128)(2,1)}, f32[1024,128]{1,0:T(8,128)S(1)}) custom-call(s32[1]{0:T(128)} %bitcast.where_ref, f32[6,64,2048]{2,1,0:T(8,128)} %refs_0_.1, f32[6,64,2048]{2,1,0:T(8,128)} %copy-done.25), custom_call_target="tpu_custom_call" | custom-call | flops 2516582400 | bytes 12582912 | tf_op jit(solution)/shard_map/prepare/pallas_call | solution.py:123
  85.9 3.6 %collective-permute-start.6 = (f32[32,2048]{1,0:T(8,128)S(1)}, f32[32,2048]{1,0:T(8,128)S(1)}, u32[]{:S(2)}, u32[]{:S(2)}) collective-permute-start(f32[32,2048]{1,0:T(8,128)S(1)} %get-tuple-element.44), channel_id=1, source_target_pairs={{0,22},{2,20},{4,18},{6,16},{8,30},{10,28},{12,26},{14,24},{16,6},... | collective-permute-start | bytes 786440 | tf_op jit(solution)/shard_map/ppermute | solution.py:412
  92.0 16.3 %collective-permute-done.4.refs_0_ = f32[32,2048]{1,0:T(8,128)S(1)} collective-permute-done((f32[32,2048]{1,0:T(8,128)S(1)}, f32[32,2048]{1,0:T(8,128)S(1)}, u32[]{:S(2)}, u32[]{:S(2)}) %collective-permute-start.4) | collective-permute-done | bytes 262176 | tf_op jit(solution)/shard_map/ppermute | solution.py:412
  109.2 5.4 %collective-permute-start.10 = (f32[32,2048]{1,0:T(8,128)S(1)}, f32[32,2048]{1,0:T(8,128)S(1)}, u32[]{:S(2)}, u32[]{:S(2)}) collective-permute-start(f32[32,2048]{1,0:T(8,128)S(1)} %get-tuple-element.48), channel_id=1, source_target_pairs={{0,20},{2,22},{4,16},{6,18},{8,28},{10,30},{12,24},{14,26},{16,4},... | collective-permute-start | bytes 786440 | tf_op jit(solution)/shard_map/ppermute | solution.py:412
  116.1 17.8 %collective-permute-done.8.refs_4_.refs_0_ = f32[32,2048]{1,0:T(8,128)S(1)} collective-permute-done((f32[32,2048]{1,0:T(8,128)S(1)}, f32[32,2048]{1,0:T(8,128)S(1)}, u32[]{:S(2)}, u32[]{:S(2)}) %collective-permute-start.8) | collective-permute-done | bytes 262176 | tf_op jit(solution)/shard_map/ppermute | solution.py:412
  133.9 3.8 %collective-permute-start.39 = (f32[64,128]{1,0:T(8,128)S(1)}, f32[64,128]{1,0:T(8,128)S(1)}, u32[]{:S(2)}, u32[]{:S(2)}) collective-permute-start(f32[64,128]{1,0:T(8,128)S(1)} %get-tuple-element.76), channel_id=1, source_target_pairs={{0,24},{2,26},{4,28},{6,30},{8,16},{10,18},{12,20},{14,22},{16,8},... | collective-permute-start | bytes 98312 | tf_op jit(solution)/shard_map/ppermute | solution.py:412
  138.7 5.4 %project.4 = (f32[128,768]{1,0:T(8,128)S(1)}, f32[128,768]{1,0:T(8,128)S(1)}) custom-call(s32[1]{0:T(128)} %bitcast.where_ref, f32[32,2048]{1,0:T(8,128)} %copy-done.11, f32[32,2048]{1,0:T(8,128)} %copy-done.12, f32[32,2048]{1,0:T(8,128)} %copy-done.13, f32[32,2048]{1,0:T(8,128)} %copy-done.14, f32[32,2048]{1,0:T(8,128)} %copy-done.15, ...), custom_call_target="tpu_custom_call" | custom-call | flops 2415919104 | bytes 10485760 | tf_op jit(solution)/shard_map/project/pallas_call | solution.py:202
  153.5 6.5 %collective-permute-done.15.refs_1_ = f32[32,2048]{1,0:T(8,128)S(1)} collective-permute-done((f32[32,2048]{1,0:T(8,128)S(1)}, f32[32,2048]{1,0:T(8,128)S(1)}, u32[]{:S(2)}, u32[]{:S(2)}) %collective-permute-start.15) | collective-permute-done | bytes 262176 | tf_op jit(solution)/shard_map/ppermute | solution.py:412
  160.0 10.4 %collective-permute-start.2 = (f32[32,2048]{1,0:T(8,128)S(1)}, f32[32,2048]{1,0:T(8,128)S(1)}, u32[]{:S(2)}, u32[]{:S(2)}) collective-permute-start(f32[32,2048]{1,0:T(8,128)S(1)} %get-tuple-element.39), channel_id=1, source_target_pairs={{0,24},{2,26},{4,28},{6,30},{8,16},{10,18},{12,20},{14,22},{16,8},... | collective-permute-start | bytes 786440 | tf_op jit(solution)/shard_map/ppermute | solution.py:412
  171.9 4.4 %project.5 = f32[128,768]{1,0:T(8,128)S(1)} custom-call(s32[1]{0:T(128)} %bitcast.where_ref, f32[32,2048]{1,0:T(8,128)} %copy-done.3, f32[32,2048]{1,0:T(8,128)} %copy-done.4, f32[32,2048]{1,0:T(8,128)} %copy-done.5, f32[32,2048]{1,0:T(8,128)} %copy-done.6, bf16[768,2048]{1,0:T(8,128)(2,1)} %get-tuple-element.40.refs_4_.refs_8_.refs_20_, ...), custom_call_target="tpu_custom_call" | custom-call | flops 1207959552 | bytes 8388608 | tf_op jit(solution)/shard_map/project/pallas_call | solution.py:202
  178.1 16.3 %collective-permute-start.42 = (f32[2,64,128]{2,1,0:T(8,128)S(1)}, f32[2,64,128]{2,1,0:T(8,128)S(1)}, u32[]{:S(2)}, u32[]{:S(2)}) collective-permute-start(f32[2,64,128]{2,1,0:T(8,128)S(1)} %get-tuple-element.79), channel_id=1, source_target_pairs={{0,16},{2,18},{4,20},{6,22},{8,24},{10,26},{12,28},{14,30},{16,0},... | collective-permute-start | bytes 196616 | tf_op jit(solution)/shard_map/ppermute | solution.py:412
  196.0 4.4 %project.3 = f32[128,768]{1,0:T(8,128)S(1)} custom-call(s32[1]{0:T(128)} %bitcast.where_ref, f32[32,2048]{1,0:T(8,128)} %copy-done.1, f32[32,2048]{1,0:T(8,128)} %copy-done.7, f32[32,2048]{1,0:T(8,128)} %copy-done.8, f32[32,2048]{1,0:T(8,128)} %copy-done.9, bf16[768,2048]{1,0:T(8,128)(2,1)} %get-tuple-element.40.refs_4_.refs_8_.refs_20_, ...), custom_call_target="tpu_custom_call" | custom-call | flops 1207959552 | bytes 8388608 | tf_op jit(solution)/shard_map/project/pallas_call | solution.py:202
  200.9 5.2 %collective-permute-start.19 = (f32[2,1,32,768]{3,2,1,0:T(8,128)S(1)}, f32[2,1,32,768]{3,2,1,0:T(8,128)S(1)}, u32[]{:S(2)}, u32[]{:S(2)}) collective-permute-start(f32[2,1,32,768]{3,2,1,0:T(8,128)S(1)} %slice.19), channel_id=1, source_target_pairs={{0,8},{2,10},{4,12},{6,14},{8,0},{10,2},{12,4},{14,6},{16,24},{18,... | collective-permute-start | bytes 589832 | tf_op jit(solution)/shard_map/ppermute | solution.py:412
  207.4 3.4 %collective-permute-done.19 = f32[2,1,32,768]{3,2,1,0:T(8,128)S(1)} collective-permute-done((f32[2,1,32,768]{3,2,1,0:T(8,128)S(1)}, f32[2,1,32,768]{3,2,1,0:T(8,128)S(1)}, u32[]{:S(2)}, u32[]{:S(2)}) %collective-permute-start.19) | collective-permute-done | bytes 196640 | tf_op jit(solution)/shard_map/ppermute | solution.py:412
  216.2 3.5 %collective-permute-start.33 = (f32[2,32,2048]{2,1,0:T(8,128)}, f32[2,32,2048]{2,1,0:T(8,128)S(1)}, u32[]{:S(2)}, u32[]{:S(2)}) collective-permute-start(f32[2,32,2048]{2,1,0:T(8,128)} %get-tuple-element.62), channel_id=1, source_target_pairs={{0,1},{1,0},{2,3},{3,2},{4,5},{5,4},{6,7},{7,6},{8,9},{9,8},{10,11... | collective-permute-start | bytes 1572872 | tf_op jit(solution)/shard_map/ppermute | solution.py:415
  220.0 4.5 %collective-permute-start.24 = (f32[32,768]{1,0:T(8,128)S(1)}, f32[32,768]{1,0:T(8,128)S(1)}, u32[]{:S(2)}, u32[]{:S(2)}) collective-permute-start(f32[32,768]{1,0:T(8,128)S(1)} %add.80), channel_id=1, source_target_pairs={{0,24},{2,26},{4,28},{6,30},{8,16},{10,18},{12,20},{14,22},{16,8},... | collective-permute-start | bytes 294920 | tf_op jit(solution)/shard_map/ppermute | solution.py:412
  229.7 3.3 %collective-permute-done.23 = f32[32,768]{1,0:T(8,128)S(1)} collective-permute-done((f32[32,768]{1,0:T(8,128)S(1)}, f32[32,768]{1,0:T(8,128)S(1)}, u32[]{:S(2)}, u32[]{:S(2)}) %collective-permute-start.23) | collective-permute-done | bytes 98336 | tf_op jit(solution)/shard_map/ppermute | solution.py:412
  241.9 3.1 %collective-permute-start.32 = (f32[2,32,2048]{2,1,0:T(8,128)}, f32[2,32,2048]{2,1,0:T(8,128)}, u32[]{:S(2)}, u32[]{:S(2)}) collective-permute-start(f32[2,32,2048]{2,1,0:T(8,128)} %get-tuple-element.61), channel_id=1, source_target_pairs={{0,1},{1,0},{2,3},{3,2},{4,5},{5,4},{6,7},{7,6},{8,9},{9,8},{10,11... | collective-permute-start | bytes 1572872 | tf_op jit(solution)/shard_map/ppermute | solution.py:415
  249.3 3.5 %factor.1 = (bf16[768,768]{1,0:T(8,128)(2,1)S(1)}, bf16[768,768]{1,0:T(8,128)(2,1)S(1)}) custom-call(f32[2,1024,128]{2,1,0:T(8,128)S(1)} %bitcast.62, f32[6,128,128]{2,1,0:T(8,128)S(1)} %copy-done.2), custom_call_target="tpu_custom_call" | custom-call | flops 1811939328 | bytes 4194304 | tf_op jit(solution)/shard_map/factor/pallas_call | solution.py:309
  252.8 5.3 %collective-permute-done.32.refs_15_ = f32[2,32,2048]{2,1,0:T(8,128)} collective-permute-done((f32[2,32,2048]{2,1,0:T(8,128)}, f32[2,32,2048]{2,1,0:T(8,128)}, u32[]{:S(2)}, u32[]{:S(2)}) %collective-permute-start.32) | collective-permute-done | bytes 524320 | tf_op jit(solution)/shard_map/ppermute | solution.py:415
  258.1 11.2 %collective-permute-done.31.refs_14_ = f32[2,32,2048]{2,1,0:T(8,128)} collective-permute-done((f32[2,32,2048]{2,1,0:T(8,128)}, f32[2,32,2048]{2,1,0:T(8,128)}, u32[]{:S(2)}, u32[]{:S(2)}) %collective-permute-start.31) | collective-permute-done | bytes 524320 | tf_op jit(solution)/shard_map/ppermute | solution.py:415
  269.3 9.6 %collective-permute-done.34.refs_17_ = f32[2,32,2048]{2,1,0:T(8,128)} collective-permute-done((f32[2,32,2048]{2,1,0:T(8,128)}, f32[2,32,2048]{2,1,0:T(8,128)}, u32[]{:S(2)}, u32[]{:S(2)}) %collective-permute-start.34) | collective-permute-done | bytes 524320 | tf_op jit(solution)/shard_map/ppermute | solution.py:415
  278.9 10.8 %apply_update.1 = f32[2,1,256,2048]{3,2,1,0:T(8,128)} custom-call(s32[1]{0:T(128)} %bitcast.where_ref, f32[1,32,768]{2,1,0:T(8,128)S(1)} %bitcast.64, f32[1,32,768]{2,1,0:T(8,128)S(1)} %bitcast.74, f32[1,32,768]{2,1,0:T(8,128)S(1)} %bitcast.72, f32[1,32,768]{2,1,0:T(8,128)S(1)} %bitcast.70, f32[4,32,768]{2,1,0:T(8,128)S(1)} %collective-permute-done.25.refs_4_, ...), custom_call_target="tpu_custom_call" | custom-call | flops 4831838208 | bytes 16252928 | tf_op jit(solution)/shard_map/apply_update/pallas_call | solution.py:370
  (155 shorter events, 54.5 us)
Async XLA Ops:
  0.0 71.3 %collective-permute-start.3 = (f32[6,64,2048]{2,1,0:T(8,128)}, f32[6,64,2048]{2,1,0:T(8,128)S(1)}, u32[]{:S(2)}, u32[]{:S(2)}) collective-permute-start(f32[6,64,2048]{2,1,0:T(8,128)} %refs_0_.1), channel_id=1, source_target_pairs={{0,1},{1,0},{2,3},{3,2},{4,5},{5,4},{6,7},{7,6},{8,9},{9,8},{10,11... | collective-permute-start | bytes 9437192 | tf_op jit(solution)/shard_map/ppermute | solution.py:415
  82.8 25.5 %collective-permute-start.4 = (f32[32,2048]{1,0:T(8,128)S(1)}, f32[32,2048]{1,0:T(8,128)S(1)}, u32[]{:S(2)}, u32[]{:S(2)}) collective-permute-start(f32[32,2048]{1,0:T(8,128)S(1)} %get-tuple-element.42), channel_id=1, source_target_pairs={{0,6},{2,4},{4,2},{6,0},{8,14},{10,12},{12,10},{14,8},{16,22},{18,... | collective-permute-start | bytes 786440 | tf_op jit(solution)/shard_map/ppermute | solution.py:412
  84.8 24.4 %collective-permute-start.5 = (f32[32,2048]{1,0:T(8,128)S(1)}, f32[32,2048]{1,0:T(8,128)S(1)}, u32[]{:S(2)}, u32[]{:S(2)}) collective-permute-start(f32[32,2048]{1,0:T(8,128)S(1)} %get-tuple-element.43), channel_id=1, source_target_pairs={{0,14},{2,12},{4,10},{6,8},{8,6},{10,4},{12,2},{14,0},{16,30},{18,... | collective-permute-start | bytes 786440 | tf_op jit(solution)/shard_map/ppermute | solution.py:412
  85.9 23.2 %collective-permute-start.6 = (f32[32,2048]{1,0:T(8,128)S(1)}, f32[32,2048]{1,0:T(8,128)S(1)}, u32[]{:S(2)}, u32[]{:S(2)}) collective-permute-start(f32[32,2048]{1,0:T(8,128)S(1)} %get-tuple-element.44), channel_id=1, source_target_pairs={{0,22},{2,20},{4,18},{6,16},{8,30},{10,28},{12,26},{14,24},{16,6},... | collective-permute-start | bytes 786440 | tf_op jit(solution)/shard_map/ppermute | solution.py:412
  89.6 24.9 %collective-permute-start.36 = (f32[4,64,128]{2,1,0:T(8,128)S(1)}, f32[4,64,128]{2,1,0:T(8,128)S(1)}, u32[]{:S(2)}, u32[]{:S(2)}) collective-permute-start(f32[4,64,128]{2,1,0:T(8,128)S(1)} %dynamic-slice_bitcast_fusion.1), channel_id=1, source_target_pairs={{0,4},{2,6},{4,0},{6,2},{8,12},{10,14},{12,8},{14,10},{16,20},{18,... | collective-permute-start | bytes 393224 | tf_op jit(solution)/shard_map/ppermute | solution.py:412
  90.2 25.8 %collective-permute-start.7 = (f32[32,2048]{1,0:T(8,128)S(1)}, f32[32,2048]{1,0:T(8,128)S(1)}, u32[]{:S(2)}, u32[]{:S(2)}) collective-permute-start(f32[32,2048]{1,0:T(8,128)S(1)} %get-tuple-element.45), channel_id=1, source_target_pairs={{0,30},{2,28},{4,26},{6,24},{8,22},{10,20},{12,18},{14,16},{16,14}... | collective-permute-start | bytes 786440 | tf_op jit(solution)/shard_map/ppermute | solution.py:412
  108.3 25.6 %collective-permute-start.8 = (f32[32,2048]{1,0:T(8,128)S(1)}, f32[32,2048]{1,0:T(8,128)S(1)}, u32[]{:S(2)}, u32[]{:S(2)}) collective-permute-start(f32[32,2048]{1,0:T(8,128)S(1)} %get-tuple-element.46), channel_id=1, source_target_pairs={{0,4},{2,6},{4,0},{6,2},{8,12},{10,14},{12,8},{14,10},{16,20},{18,... | collective-permute-start | bytes 786440 | tf_op jit(solution)/shard_map/ppermute | solution.py:412
  109.1 28.6 %collective-permute-start.9 = (f32[32,2048]{1,0:T(8,128)S(1)}, f32[32,2048]{1,0:T(8,128)S(1)}, u32[]{:S(2)}, u32[]{:S(2)}) collective-permute-start(f32[32,2048]{1,0:T(8,128)S(1)} %get-tuple-element.47), channel_id=1, source_target_pairs={{0,12},{2,14},{4,8},{6,10},{8,4},{10,6},{12,0},{14,2},{16,28},{18,... | collective-permute-start | bytes 786440 | tf_op jit(solution)/shard_map/ppermute | solution.py:412
  109.2 28.6 %collective-permute-start.10 = (f32[32,2048]{1,0:T(8,128)S(1)}, f32[32,2048]{1,0:T(8,128)S(1)}, u32[]{:S(2)}, u32[]{:S(2)}) collective-permute-start(f32[32,2048]{1,0:T(8,128)S(1)} %get-tuple-element.48), channel_id=1, source_target_pairs={{0,20},{2,22},{4,16},{6,18},{8,28},{10,30},{12,24},{14,26},{16,4},... | collective-permute-start | bytes 786440 | tf_op jit(solution)/shard_map/ppermute | solution.py:412
  114.5 23.3 %collective-permute-start.11 = (f32[32,2048]{1,0:T(8,128)S(1)}, f32[32,2048]{1,0:T(8,128)S(1)}, u32[]{:S(2)}, u32[]{:S(2)}) collective-permute-start(f32[32,2048]{1,0:T(8,128)S(1)} %get-tuple-element.49), channel_id=1, source_target_pairs={{0,28},{2,30},{4,24},{6,26},{8,20},{10,22},{12,16},{14,18},{16,12}... | collective-permute-start | bytes 786440 | tf_op jit(solution)/shard_map/ppermute | solution.py:412
  116.0 30.1 %collective-permute-start.37 = (f32[64,128]{1,0:T(8,128)S(1)}, f32[64,128]{1,0:T(8,128)S(1)}, u32[]{:S(2)}, u32[]{:S(2)}) collective-permute-start(f32[64,128]{1,0:T(8,128)S(1)} %get-tuple-element.75), channel_id=1, source_target_pairs={{0,8},{2,10},{4,12},{6,14},{8,0},{10,2},{12,4},{14,6},{16,24},{18,... | collective-permute-start | bytes 98312 | tf_op jit(solution)/shard_map/ppermute | solution.py:412
  144.2 32.2 %collective-permute-start.12 = (f32[128,768]{1,0:T(8,128)S(1)}, f32[128,768]{1,0:T(8,128)S(1)}, u32[]{:S(2)}, u32[]{:S(2)}) collective-permute-start(f32[128,768]{1,0:T(8,128)S(1)} %get-tuple-element.51), channel_id=1, source_target_pairs={{0,2},{2,0},{4,6},{6,4},{8,10},{10,8},{12,14},{14,12},{16,18},{18,... | collective-permute-start | bytes 1179656 | tf_op jit(solution)/shard_map/ppermute | solution.py:412
  152.8 25.3 %collective-permute-start = (f32[32,2048]{1,0:T(8,128)S(1)}, f32[32,2048]{1,0:T(8,128)S(1)}, u32[]{:S(2)}, u32[]{:S(2)}) collective-permute-start(f32[32,2048]{1,0:T(8,128)S(1)} %get-tuple-element.37), channel_id=1, source_target_pairs={{0,8},{2,10},{4,12},{6,14},{8,0},{10,2},{12,4},{14,6},{16,24},{18,... | collective-permute-start | bytes 786440 | tf_op jit(solution)/shard_map/ppermute | solution.py:412
  160.0 34.4 %collective-permute-start.1 = (f32[32,2048]{1,0:T(8,128)S(1)}, f32[32,2048]{1,0:T(8,128)S(1)}, u32[]{:S(2)}, u32[]{:S(2)}) collective-permute-start(f32[32,2048]{1,0:T(8,128)S(1)} %get-tuple-element.38), channel_id=1, source_target_pairs={{0,16},{2,18},{4,20},{6,22},{8,24},{10,26},{12,28},{14,30},{16,0},... | collective-permute-start | bytes 786440 | tf_op jit(solution)/shard_map/ppermute | solution.py:412
  160.0 34.4 %collective-permute-start.2 = (f32[32,2048]{1,0:T(8,128)S(1)}, f32[32,2048]{1,0:T(8,128)S(1)}, u32[]{:S(2)}, u32[]{:S(2)}) collective-permute-start(f32[32,2048]{1,0:T(8,128)S(1)} %get-tuple-element.39), channel_id=1, source_target_pairs={{0,24},{2,26},{4,28},{6,30},{8,16},{10,18},{12,20},{14,22},{16,8},... | collective-permute-start | bytes 786440 | tf_op jit(solution)/shard_map/ppermute | solution.py:412
  176.3 24.4 %collective-permute-start.18 = (f32[128,768]{1,0:T(8,128)S(1)}, f32[128,768]{1,0:T(8,128)S(1)}, u32[]{:S(2)}, u32[]{:S(2)}) collective-permute-start(f32[128,768]{1,0:T(8,128)S(1)} %project.5), channel_id=1, source_target_pairs={{0,2},{2,0},{4,6},{6,4},{8,10},{10,8},{12,14},{14,12},{16,18},{18,... | collective-permute-start | bytes 1179656 | tf_op jit(solution)/shard_map/ppermute | solution.py:412
  176.9 23.9 %collective-permute-start.13 = (f32[128,768]{1,0:T(8,128)S(1)}, f32[128,768]{1,0:T(8,128)S(1)}, u32[]{:S(2)}, u32[]{:S(2)}) collective-permute-start(f32[128,768]{1,0:T(8,128)S(1)} %add.76), channel_id=1, source_target_pairs={{0,4},{2,6},{4,0},{6,2},{8,12},{10,14},{12,8},{14,10},{16,20},{18,... | collective-permute-start | bytes 1179656 | tf_op jit(solution)/shard_map/ppermute | solution.py:412
  178.1 22.3 %collective-permute-start.42 = (f32[2,64,128]{2,1,0:T(8,128)S(1)}, f32[2,64,128]{2,1,0:T(8,128)S(1)}, u32[]{:S(2)}, u32[]{:S(2)}) collective-permute-start(f32[2,64,128]{2,1,0:T(8,128)S(1)} %get-tuple-element.79), channel_id=1, source_target_pairs={{0,16},{2,18},{4,20},{6,22},{8,24},{10,26},{12,28},{14,30},{16,0},... | collective-permute-start | bytes 196616 | tf_op jit(solution)/shard_map/ppermute | solution.py:412
  216.2 32.4 %collective-permute-start.33 = (f32[2,32,2048]{2,1,0:T(8,128)}, f32[2,32,2048]{2,1,0:T(8,128)S(1)}, u32[]{:S(2)}, u32[]{:S(2)}) collective-permute-start(f32[2,32,2048]{2,1,0:T(8,128)} %get-tuple-element.62), channel_id=1, source_target_pairs={{0,1},{1,0},{2,3},{3,2},{4,5},{5,4},{6,7},{7,6},{8,9},{9,8},{10,11... | collective-permute-start | bytes 1572872 | tf_op jit(solution)/shard_map/ppermute | solution.py:415
  219.9 28.7 %collective-permute-start.45 = (f32[8,2,64,128]{3,2,0,1:T(8,128)S(1)}, f32[8,2,64,128]{3,2,0,1:T(8,128)S(1)}, u32[]{:S(2)}, u32[]{:S(2)}) collective-permute-start(f32[8,2,64,128]{3,2,0,1:T(8,128)S(1)} %bitcast.81), channel_id=1, source_target_pairs={{0,2},{2,0},{4,6},{6,4},{8,10},{10,8},{12,14},{14,12},{16,18},{18,... | collective-permute-start | bytes 1572872 | tf_op jit(solution)/shard_map/ppermute | solution.py:412
  245.0 24.3 %collective-permute-start.31 = (f32[2,32,2048]{2,1,0:T(8,128)}, f32[2,32,2048]{2,1,0:T(8,128)}, u32[]{:S(2)}, u32[]{:S(2)}) collective-permute-start(f32[2,32,2048]{2,1,0:T(8,128)} %get-tuple-element.60), channel_id=1, source_target_pairs={{0,1},{1,0},{2,3},{3,2},{4,5},{5,4},{6,7},{7,6},{8,9},{9,8},{10,11... | collective-permute-start | bytes 1572872 | tf_op jit(solution)/shard_map/ppermute | solution.py:415
  245.1 33.8 %collective-permute-start.34 = (f32[2,32,2048]{2,1,0:T(8,128)}, f32[2,32,2048]{2,1,0:T(8,128)}, u32[]{:S(2)}, u32[]{:S(2)}) collective-permute-start(f32[2,32,2048]{2,1,0:T(8,128)} %get-tuple-element.63), channel_id=1, source_target_pairs={{0,1},{1,0},{2,3},{3,2},{4,5},{5,4},{6,7},{7,6},{8,9},{9,8},{10,11... | collective-permute-start | bytes 1572872 | tf_op jit(solution)/shard_map/ppermute | solution.py:415
  248.6 30.2 %collective-permute-start.25 = (f32[4,32,768]{2,1,0:T(8,128)}, f32[4,32,768]{2,1,0:T(8,128)S(1)}, u32[]{:S(2)}, u32[]{:S(2)}) collective-permute-start(f32[4,32,768]{2,1,0:T(8,128)} %pad_maximum_fusion), channel_id=1, source_target_pairs={{0,2},{2,0},{4,6},{6,4},{8,10},{10,8},{12,14},{14,12},{16,18},{18,... | collective-permute-start | bytes 1179656 | tf_op jit(solution)/shard_map/ppermute | solution.py:412
  248.6 30.2 %collective-permute-start.30 = (f32[4,32,768]{2,1,0:T(8,128)}, f32[4,32,768]{2,1,0:T(8,128)S(1)}, u32[]{:S(2)}, u32[]{:S(2)}) collective-permute-start(f32[4,32,768]{2,1,0:T(8,128)} %pad_maximum_fusion.1), channel_id=1, source_target_pairs={{0,2},{2,0},{4,6},{6,4},{8,10},{10,8},{12,14},{14,12},{16,18},{18,... | collective-permute-start | bytes 1179656 | tf_op jit(solution)/shard_map/ppermute | solution.py:412
  (48 other events, 470.3 us)
